TPU v7x, 32 devices: a whole 2x2x4 slice. The times are simulated.
32 devices in a mesh: seq: 8 (over z, y), head: 4 (over x, core).
Axes of the slice: x: 2, y: 2, z: 4, core: 2. Of those that a mesh axis runs over, the one named last changes fastest.
Arguments:
- queries: bfloat16 [4096, 512], P('seq', 'head'), may hold values from -4.5 to 4.5
- keys: bfloat16 [4096, 512], P('seq', 'head'), may hold values from -4.5 to 4.5
- values: bfloat16 [4096, 512], P('seq', 'head'), may hold values from -6 to 6
- grad_out: bfloat16 [4096, 512], P('seq', 'head'), may hold values from -6 to 6
- block_perm: int32 [4, 8], P('head'), may hold values from 0 to 7, as said below
Outputs:
- attended: bfloat16 [4096, 512], P('seq', 'head')
- grad_queries: bfloat16 [4096, 512], P('seq', 'head')
- grad_keys: bfloat16 [4096, 512], P('seq', 'head')
- grad_values: bfloat16 [4096, 512], P('seq', 'head')
Inputs may be any that keep to these rules, and one draw needn't show every extreme that they name: Each row of block_perm is a permutation of 0 to 7.
All inputs are finite; a program needn't handle non-finite values.
Results may differ from a plain program's by a relative error of at most 0.007.
Values may be sent and summed in bfloat16 or wider, within the bound.
No kernel may reach another device: no remote copies, remote signals or barrier semaphores. Data moves between devices by JAX's collectives and lax.ppermute only.
A program may use at most 64 MiB of HBM per device.

v0:
```python
import jax
import jax.numpy as jnp
from jax import lax
from jax.sharding import PartitionSpec as P

BLK = 512


def from_partner(value, axis, apart):
    mask = 2**apart
    pairs = [(source, source ^ mask) for source in range(lax.axis_size(axis))]
    return lax.ppermute(value, axis, pairs)


def passed_along(value, axis, steps):
    count = lax.axis_size(axis)
    first, last = (max(0, -steps), min(count, count - steps))
    return lax.ppermute(value, axis, [(source, source + steps) for source in range(first, last)])


def window_block(query_rows, window, grad_rows, has_prev):
    width = query_rows.shape[1]
    span = query_rows.shape[0]
    scale = width ** (-0.5)
    win_keys = window[:, :width]
    win_values = window[:, width:]
    scores = jnp.dot(query_rows, win_keys.T, preferred_element_type=jnp.float32) * scale
    column = jnp.arange(window.shape[0], dtype=jnp.int32)
    allowed = jnp.logical_or(column >= span, has_prev)
    scores = jnp.where(allowed[None, :], scores, -1e30)
    top = jnp.max(scores, axis=1, keepdims=True)
    expon = jnp.exp(scores - top)
    probs = expon / jnp.sum(expon, axis=1, keepdims=True)
    probs_low = probs.astype(jnp.bfloat16)
    attended = jnp.dot(probs_low, win_values, preferred_element_type=jnp.float32).astype(
        jnp.bfloat16
    )
    grad_probs = jnp.dot(grad_rows, win_values.T, preferred_element_type=jnp.float32)
    delta = jnp.sum(probs * grad_probs, axis=1, keepdims=True)
    grad_scores = (probs * (grad_probs - delta) * scale).astype(jnp.bfloat16)
    grad_query = jnp.dot(grad_scores, win_keys, preferred_element_type=jnp.float32).astype(
        jnp.bfloat16
    )
    grad_key = jnp.dot(grad_scores.T, query_rows, preferred_element_type=jnp.float32)
    grad_value = jnp.dot(probs_low.T, grad_rows, preferred_element_type=jnp.float32)
    window_grads = jnp.concatenate([grad_key, grad_value], axis=1).astype(jnp.bfloat16)
    return (attended, grad_query, window_grads)


def device_bit(bit_number, low_bits):
    offset = bit_number - low_bits
    return offset


def sort_sections(perm_row, seq_index, blocks_here, low_bits, halvings):
    block_count = perm_row.shape[0]
    element_ids = jnp.arange(block_count, dtype=jnp.int32)

    def position(block_ids):
        return block_ids % blocks_here + blocks_here * (block_ids // blocks_here)

    inverse = jnp.zeros((block_count,), jnp.int32).at[perm_row].set(element_ids)
    keys_now = jnp.zeros((block_count,), jnp.int32).at[position(element_ids)].set(position(inverse))
    my_places = jnp.arange(blocks_here, dtype=jnp.int32) + blocks_here * seq_index
    section_list = []
    for section_level in range(1, low_bits + halvings + 1):
        for bit_number in range(section_level - 1, -1, -1):
            partner_keys = jnp.take(keys_now, jnp.bitwise_xor(element_ids, 1 << bit_number))
            rising = jnp.right_shift(element_ids, section_level) % 2 == 0
            low_side = jnp.right_shift(element_ids, bit_number) % 2 == 0
            kept_keys = jnp.where(
                rising == low_side,
                jnp.minimum(keys_now, partner_keys),
                jnp.maximum(keys_now, partner_keys),
            )
            moved_flags = kept_keys != keys_now
            section_list.append((bit_number, jnp.take(moved_flags, my_places)))
            keys_now = kept_keys
    return section_list


def route_blocks(blocks, section_list, low_bits, returning):
    ordered = list(reversed(section_list)) if returning else section_list
    for bit_number, moved_flags in ordered:
        if returning:
            partner_blocks = from_partner(blocks, "seq", device_bit(bit_number, low_bits))
        else:
            partner_blocks = from_partner(blocks, "seq", device_bit(bit_number, low_bits))
        blocks = jnp.where(moved_flags[:, None, None], partner_blocks, blocks)
    return blocks


def body(queries, keys, values, grad_out, block_perm):
    width = queries.shape[1]
    blocks_here = queries.shape[0] // BLK
    halvings = lax.axis_size("seq").bit_length() - 1
    low_bits = blocks_here.bit_length() - 1
    seq_index = lax.axis_index("seq")
    query_blocks = queries.reshape(blocks_here, BLK, width)
    grad_blocks = grad_out.reshape(blocks_here, BLK, width)
    pair = jnp.concatenate(
        [keys.reshape(blocks_here, BLK, width), values.reshape(blocks_here, BLK, width)], axis=2
    )
    section_list = sort_sections(block_perm[0], seq_index, blocks_here, low_bits, halvings)
    slot_ids = jnp.arange(blocks_here, dtype=jnp.int32)
    prev_pair = passed_along(pair[blocks_here - 1], "seq", 1)
    far_pair = route_blocks(pair, section_list, low_bits, False)
    previous = jnp.concatenate([prev_pair[None], pair[:-1]], axis=0)
    windows = jnp.concatenate([previous, pair, far_pair], axis=1)
    has_prev = seq_index * blocks_here + slot_ids > 0

    def one_block(items):
        return window_block(items[0], items[1], items[2], items[3])

    attended, grad_query, window_grads = lax.map(
        one_block, (query_blocks, windows, grad_blocks, has_prev)
    )
    far_back = route_blocks(window_grads[:, 2 * BLK :], section_list, low_bits, True)
    prev_back = passed_along(window_grads[0, :BLK], "seq", -1)
    local_part = window_grads[:, BLK : 2 * BLK].astype(jnp.float32)
    prev_moved = jnp.concatenate([window_grads[1:, :BLK], prev_back[None]], axis=0).astype(
        jnp.float32
    )
    far_moved = far_back.astype(jnp.float32)
    total = (
        (local_part + prev_moved + far_moved)
        .astype(jnp.bfloat16)
        .reshape(blocks_here * BLK, 2 * width)
    )
    return (
        attended.reshape(blocks_here * BLK, width),
        grad_query.reshape(blocks_here * BLK, width),
        total[:, :width],
        total[:, width:],
    )


def solution(mesh):
    placed = (
        P("seq", "head"),
        P("seq", "head"),
        P("seq", "head"),
        P("seq", "head"),
        P("head", None),
    )
    return jax.shard_map(
        body,
        mesh=mesh,
        in_specs=placed,
        out_specs=(P("seq", "head"), P("seq", "head"), P("seq", "head"), P("seq", "head")),
        check_vma=False,
    )
```

profile of v0, /device:TPU:0, one launch (start us, length us, event | category | flops | bytes accessed | tf_op | source)
XLA Modules:
  0.0 111.4 jit_solution(3158085258241841003)
XLA Ops:
  0.6 0.0 copy-start
  0.6 1.0 copy.14
  1.7 1.0 copy.13
  2.7 3.1 %collective-permute-start.1 = (bf16[1,512,256]{1,2,0:T(8,128)(2,1)S(1)}, bf16[1,512,256]{1,2,0:T(8,128)(2,1)S(1)}, u32[]{:S(2)}, u32[]{:S(2)}) collective-permute-start(bf16[1,512,256]{1,2,0:T(8,128)(2,1)S(1)} %pad_maximum_fusion.1), channel_id=1, source_target_pairs={{0,4},{4,0},{8,12},{12,8},{16,20},{20,16},{24,28},{28,24},{1,5},{5... | collective-permute-start | bytes 786440 | tf_op jit(solution)/shard_map/ppermute | solution.py:12
  5.8 0.7 fusion.28
  6.5 0.6 scatter_custom_fusion
  7.1 0.6 scatter_custom_fusion.1
  7.7 0.6 gather_fusion
  8.4 0.6 dynamic-slice.19
  9.6 2.5 %collective-permute-done.1 = bf16[1,512,256]{1,2,0:T(8,128)(2,1)S(1)} collective-permute-done((bf16[1,512,256]{1,2,0:T(8,128)(2,1)S(1)}, bf16[1,512,256]{1,2,0:T(8,128)(2,1)S(1)}, u32[]{:S(2)}, u32[]{:S(2)}) %collective-permute-start.1) | collective-permute-done | bytes 262176 | tf_op jit(solution)/shard_map/ppermute | solution.py:12
  12.1 0.1 fusion.33
  12.2 1.9 %collective-permute-start.2 = (bf16[1,512,256]{1,2,0:T(8,128)(2,1)S(1)}, bf16[1,512,256]{1,2,0:T(8,128)(2,1)S(1)}, u32[]{:S(2)}, u32[]{:S(2)}) collective-permute-start(bf16[1,512,256]{1,2,0:T(8,128)(2,1)S(1)} %get-tuple-element.118), channel_id=1, source_target_pairs={{0,8},{4,12},{8,0},{12,4},{16,24},{20,28},{24,16},{28,20},{1,9},{5... | collective-permute-start | bytes 786440 | tf_op jit(solution)/shard_map/ppermute | solution.py:12
  14.0 0.6 gather_fusion.1
  14.7 0.6 dynamic-slice.18
  16.0 0.6 gather_fusion.2
  16.6 3.1 %collective-permute-done.2 = bf16[1,512,256]{1,2,0:T(8,128)(2,1)S(1)} collective-permute-done((bf16[1,512,256]{1,2,0:T(8,128)(2,1)S(1)}, bf16[1,512,256]{1,2,0:T(8,128)(2,1)S(1)}, u32[]{:S(2)}, u32[]{:S(2)}) %collective-permute-start.2) | collective-permute-done | bytes 262176 | tf_op jit(solution)/shard_map/ppermute | solution.py:12
  19.7 1.5 %collective-permute-start.3 = (bf16[1,512,256]{1,2,0:T(8,128)(2,1)S(1)}, bf16[1,512,256]{1,2,0:T(8,128)(2,1)S(1)}, u32[]{:S(2)}, u32[]{:S(2)}) collective-permute-start(bf16[1,512,256]{1,2,0:T(8,128)(2,1)S(1)} %broadcast_select_fusion.2), channel_id=1, source_target_pairs={{0,4},{4,0},{8,12},{12,8},{16,20},{20,16},{24,28},{28,24},{1,5},{5... | collective-permute-start | bytes 786440 | tf_op jit(solution)/shard_map/ppermute | solution.py:12
  21.3 0.6 dynamic-slice.17
  22.5 3.9 %collective-permute-done.3 = bf16[1,512,256]{1,2,0:T(8,128)(2,1)S(1)} collective-permute-done((bf16[1,512,256]{1,2,0:T(8,128)(2,1)S(1)}, bf16[1,512,256]{1,2,0:T(8,128)(2,1)S(1)}, u32[]{:S(2)}, u32[]{:S(2)}) %collective-permute-start.3) | collective-permute-done | bytes 262176 | tf_op jit(solution)/shard_map/ppermute | solution.py:12
  26.4 0.0 copy-start.1
  26.5 2.4 %collective-permute-start.4 = (bf16[1,512,256]{1,2,0:T(8,128)(2,1)S(1)}, bf16[1,512,256]{1,2,0:T(8,128)(2,1)S(1)}, u32[]{:S(2)}, u32[]{:S(2)}) collective-permute-start(bf16[1,512,256]{1,2,0:T(8,128)(2,1)S(1)} %broadcast_select_fusion.4), channel_id=1, source_target_pairs={{0,16},{4,20},{8,24},{12,28},{16,0},{20,4},{24,8},{28,12},{1,17},{... | collective-permute-start | bytes 786440 | tf_op jit(solution)/shard_map/ppermute | solution.py:12
  28.8 0.6 gather_fusion.3
  29.5 0.6 dynamic-slice.16
  30.8 8.1 %collective-permute-done.4 = bf16[1,512,256]{1,2,0:T(8,128)(2,1)S(1)} collective-permute-done((bf16[1,512,256]{1,2,0:T(8,128)(2,1)S(1)}, bf16[1,512,256]{1,2,0:T(8,128)(2,1)S(1)}, u32[]{:S(2)}, u32[]{:S(2)}) %collective-permute-start.4) | collective-permute-done | bytes 262176 | tf_op jit(solution)/shard_map/ppermute | solution.py:12
  38.8 0.1 collective-permute-start.5
  38.9 0.6 gather_fusion.4
  39.6 0.6 dynamic-slice.15
  40.8 0.6 gather_fusion.5
  41.5 5.1 %collective-permute-done.5 = bf16[1,512,256]{1,2,0:T(8,128)(2,1)S(1)} collective-permute-done((bf16[1,512,256]{1,2,0:T(8,128)(2,1)S(1)}, bf16[1,512,256]{1,2,0:T(8,128)(2,1)S(1)}, u32[]{:S(2)}, u32[]{:S(2)}) %collective-permute-start.5) | collective-permute-done | bytes 262176 | tf_op jit(solution)/shard_map/ppermute | solution.py:12
  46.6 0.1 collective-permute-start.6
  46.8 3.9 %collective-permute-start = (bf16[512,256]{0,1:T(8,128)(2,1)S(1)}, bf16[512,256]{0,1:T(8,128)(2,1)S(1)}, u32[]{:S(2)}, u32[]{:S(2)}) collective-permute-start(bf16[512,256]{0,1:T(8,128)(2,1)S(1)} %get-tuple-element.117), channel_id=1, source_target_pairs={{0,4},{4,8},{8,12},{12,16},{16,20},{20,24},{24,28},{1,5},{5,9},{9,... | collective-permute-start | bytes 786440 | tf_op jit(solution)/shard_map/ppermute | solution.py:18
  50.7 0.7 dynamic-slice.14
  52.0 1.6 %collective-permute-done.6 = bf16[1,512,256]{1,2,0:T(8,128)(2,1)S(1)} collective-permute-done((bf16[1,512,256]{1,2,0:T(8,128)(2,1)S(1)}, bf16[1,512,256]{1,2,0:T(8,128)(2,1)S(1)}, u32[]{:S(2)}, u32[]{:S(2)}) %collective-permute-start.6) | collective-permute-done | bytes 262176 | tf_op jit(solution)/shard_map/ppermute | solution.py:12
  53.6 3.4 %collective-permute-done = bf16[512,256]{0,1:T(8,128)(2,1)S(1)} collective-permute-done((bf16[512,256]{0,1:T(8,128)(2,1)S(1)}, bf16[512,256]{0,1:T(8,128)(2,1)S(1)}, u32[]{:S(2)}, u32[]{:S(2)}) %collective-permute-start) | collective-permute-done | bytes 262176 | tf_op jit(solution)/shard_map/ppermute | solution.py:18
  57.0 0.1 maximum_bitcast_fusion
  57.0 0.0 copy-done.1
  57.1 1.3 %fusion.42 = (f32[512]{0:T(512)S(1)}, f32[1536,512]{1,0:T(8,128)S(1)}) fusion(bf16[512,128]{1,0:T(8,128)(2,1)S(1)} %copy-done.1, bf16[1536,256]{0,1:T(8,128)(2,1)S(1)} %maximum_bitcast_fusion, pred[1536]{0:T(1024)(128)(4,1)S(1)} %fusion.18), kind=kOutput, calls=%fused_computation.108 | convolution fusion | flops 203685376 | bytes 3674112 | tf_op jit(solution)/shard_map/while/body/eval_jaxpr/dot_general | solution.py:27
  58.4 0.5 fusion.4
  58.9 0.0 copy-done
  58.9 0.8 fusion.1
  59.6 0.7 fusion.7
  60.4 0.9 fusion.3
  61.2 0.6 fusion.6
  61.9 2.5 %collective-permute-start.8 = (bf16[1,512,256]{1,2,0:T(8,128)(2,1)S(1)}, bf16[1,512,256]{1,2,0:T(8,128)(2,1)S(1)}, u32[]{:S(2)}, u32[]{:S(2)}) collective-permute-start(bf16[1,512,256]{1,2,0:T(8,128)(2,1)S(1)} %get-tuple-element.113), channel_id=1, source_target_pairs={{0,4},{4,0},{8,12},{12,8},{16,20},{20,16},{24,28},{28,24},{1,5},{5... | collective-permute-start | bytes 786440 | tf_op jit(solution)/shard_map/ppermute | solution.py:12
  64.5 4.5 %collective-permute-done.8 = bf16[1,512,256]{1,2,0:T(8,128)(2,1)S(1)} collective-permute-done((bf16[1,512,256]{1,2,0:T(8,128)(2,1)S(1)}, bf16[1,512,256]{1,2,0:T(8,128)(2,1)S(1)}, u32[]{:S(2)}, u32[]{:S(2)}) %collective-permute-start.8) | collective-permute-done | bytes 262176 | tf_op jit(solution)/shard_map/ppermute | solution.py:12
  69.0 2.3 %collective-permute-start.9 = (bf16[1,512,256]{1,2,0:T(8,128)(2,1)S(1)}, bf16[1,512,256]{1,2,0:T(8,128)(2,1)S(1)}, u32[]{:S(2)}, u32[]{:S(2)}) collective-permute-start(bf16[1,512,256]{1,2,0:T(8,128)(2,1)S(1)} %broadcast_select_fusion.9), channel_id=1, source_target_pairs={{0,8},{4,12},{8,0},{12,4},{16,24},{20,28},{24,16},{28,20},{1,9},{5... | collective-permute-start | bytes 786440 | tf_op jit(solution)/shard_map/ppermute | solution.py:12
  71.3 6.6 %collective-permute-done.9 = bf16[1,512,256]{1,2,0:T(8,128)(2,1)S(1)} collective-permute-done((bf16[1,512,256]{1,2,0:T(8,128)(2,1)S(1)}, bf16[1,512,256]{1,2,0:T(8,128)(2,1)S(1)}, u32[]{:S(2)}, u32[]{:S(2)}) %collective-permute-start.9) | collective-permute-done | bytes 262176 | tf_op jit(solution)/shard_map/ppermute | solution.py:12
  77.9 0.5 collective-permute-start.10
  78.4 9.7 %collective-permute-done.10 = bf16[1,512,256]{1,2,0:T(8,128)(2,1)S(1)} collective-permute-done((bf16[1,512,256]{1,2,0:T(8,128)(2,1)S(1)}, bf16[1,512,256]{1,2,0:T(8,128)(2,1)S(1)}, u32[]{:S(2)}, u32[]{:S(2)}) %collective-permute-start.10) | collective-permute-done | bytes 262176 | tf_op jit(solution)/shard_map/ppermute | solution.py:12
  88.1 0.3 collective-permute-start.11
  88.5 8.3 %collective-permute-done.11 = bf16[1,512,256]{1,2,0:T(8,128)(2,1)S(1)} collective-permute-done((bf16[1,512,256]{1,2,0:T(8,128)(2,1)S(1)}, bf16[1,512,256]{1,2,0:T(8,128)(2,1)S(1)}, u32[]{:S(2)}, u32[]{:S(2)}) %collective-permute-start.11) | collective-permute-done | bytes 262176 | tf_op jit(solution)/shard_map/ppermute | solution.py:12
  96.8 0.1 collective-permute-start.12
  96.9 1.3 %convolution_convert_fusion.3 = bf16[512,128]{1,0:T(8,128)(2,1)} fusion(bf16[1536,256]{0,1:T(8,128)(2,1)S(1)} %maximum_bitcast_fusion, f32[1536,512]{1,0:T(8,128)S(1)} %get-tuple-element.120, f32[512]{0:T(512)S(1)} %fusion.4, f32[512]{0:T(512)S(1)} %get-tuple-element.119), kind=kOutput, calls=%fused_computation.25 | convolution fusion | flops 203751424 | bytes 3674112 | tf_op jit(solution)/shard_map/while/body/eval_jaxpr/dot_general | solution.py:35
  98.2 1.3 %collective-permute-start.7 = (bf16[512,256]{0,1:T(8,128)(2,1)S(1)}, bf16[512,256]{0,1:T(8,128)(2,1)S(1)}, u32[]{:S(2)}, u32[]{:S(2)}) collective-permute-start(bf16[512,256]{0,1:T(8,128)(2,1)S(1)} %get-tuple-element.114), channel_id=1, source_target_pairs={{4,0},{8,4},{12,8},{16,12},{20,16},{24,20},{28,24},{5,1},{9,5},{13... | collective-permute-start | bytes 786440 | tf_op jit(solution)/shard_map/ppermute | solution.py:18
  99.5 3.7 %collective-permute-done.12 = bf16[1,512,256]{1,2,0:T(8,128)(2,1)S(1)} collective-permute-done((bf16[1,512,256]{1,2,0:T(8,128)(2,1)S(1)}, bf16[1,512,256]{1,2,0:T(8,128)(2,1)S(1)}, u32[]{:S(2)}, u32[]{:S(2)}) %collective-permute-start.12) | collective-permute-done | bytes 262176 | tf_op jit(solution)/shard_map/ppermute | solution.py:12
  103.3 1.2 %collective-permute-start.13 = (bf16[1,512,256]{1,2,0:T(8,128)(2,1)S(1)}, bf16[1,512,256]{1,2,0:T(8,128)(2,1)S(1)}, u32[]{:S(2)}, u32[]{:S(2)}) collective-permute-start(bf16[1,512,256]{1,2,0:T(8,128)(2,1)S(1)} %broadcast_select_fusion.1), channel_id=1, source_target_pairs={{0,4},{4,0},{8,12},{12,8},{16,20},{20,16},{24,28},{28,24},{1,5},{5... | collective-permute-start | bytes 786440 | tf_op jit(solution)/shard_map/ppermute | solution.py:12
  104.4 1.3 %convolution_convert_fusion.2 = bf16[512,128]{1,0:T(8,128)(2,1)} fusion(bf16[512,1536]{0,1:T(8,128)(2,1)S(1)} %fusion.3, bf16[1536,256]{0,1:T(8,128)(2,1)S(1)} %maximum_bitcast_fusion), kind=kOutput, calls=%fused_computation.24 | convolution fusion | flops 201392128 | bytes 2097152 | tf_op jit(solution)/shard_map/while/body/eval_jaxpr/dot_general | solution.py:41
  105.7 0.8 collective-permute-done.7
  106.5 3.2 %collective-permute-done.13 = bf16[1,512,256]{1,2,0:T(8,128)(2,1)S(1)} collective-permute-done((bf16[1,512,256]{1,2,0:T(8,128)(2,1)S(1)}, bf16[1,512,256]{1,2,0:T(8,128)(2,1)S(1)}, u32[]{:S(2)}, u32[]{:S(2)}) %collective-permute-start.13) | collective-permute-done | bytes 262176 | tf_op jit(solution)/shard_map/ppermute | solution.py:12
  109.7 0.1 fusion.14
  109.9 0.8 copy.15
  110.6 0.8 copy.16
  (28 shorter events, 0.5 us)
Async XLA Ops:
  0.6 58.2 %copy-start = (bf16[512,128]{1,0:T(8,128)(2,1)S(1)}, bf16[512,128]{1,0:T(8,128)(2,1)}, u32[]{:S(2)}) copy-start(bf16[512,128]{1,0:T(8,128)(2,1)} %param.10) | copy-start | bytes 393220
  2.7 9.4 %collective-permute-start.1 = (bf16[1,512,256]{1,2,0:T(8,128)(2,1)S(1)}, bf16[1,512,256]{1,2,0:T(8,128)(2,1)S(1)}, u32[]{:S(2)}, u32[]{:S(2)}) collective-permute-start(bf16[1,512,256]{1,2,0:T(8,128)(2,1)S(1)} %pad_maximum_fusion.1), channel_id=1, source_target_pairs={{0,4},{4,0},{8,12},{12,8},{16,20},{20,16},{24,28},{28,24},{1,5},{5... | collective-permute-start | bytes 786440 | tf_op jit(solution)/shard_map/ppermute | solution.py:12
  12.2 7.5 %collective-permute-start.2 = (bf16[1,512,256]{1,2,0:T(8,128)(2,1)S(1)}, bf16[1,512,256]{1,2,0:T(8,128)(2,1)S(1)}, u32[]{:S(2)}, u32[]{:S(2)}) collective-permute-start(bf16[1,512,256]{1,2,0:T(8,128)(2,1)S(1)} %get-tuple-element.118), channel_id=1, source_target_pairs={{0,8},{4,12},{8,0},{12,4},{16,24},{20,28},{24,16},{28,20},{1,9},{5... | collective-permute-start | bytes 786440 | tf_op jit(solution)/shard_map/ppermute | solution.py:12
  19.7 6.7 %collective-permute-start.3 = (bf16[1,512,256]{1,2,0:T(8,128)(2,1)S(1)}, bf16[1,512,256]{1,2,0:T(8,128)(2,1)S(1)}, u32[]{:S(2)}, u32[]{:S(2)}) collective-permute-start(bf16[1,512,256]{1,2,0:T(8,128)(2,1)S(1)} %broadcast_select_fusion.2), channel_id=1, source_target_pairs={{0,4},{4,0},{8,12},{12,8},{16,20},{20,16},{24,28},{28,24},{1,5},{5... | collective-permute-start | bytes 786440 | tf_op jit(solution)/shard_map/ppermute | solution.py:12
  26.4 30.6 %copy-start.1 = (bf16[512,128]{1,0:T(8,128)(2,1)S(1)}, bf16[512,128]{1,0:T(8,128)(2,1)}, u32[]{:S(2)}) copy-start(bf16[512,128]{1,0:T(8,128)(2,1)} %param.7) | copy-start | bytes 393220
  26.5 12.3 %collective-permute-start.4 = (bf16[1,512,256]{1,2,0:T(8,128)(2,1)S(1)}, bf16[1,512,256]{1,2,0:T(8,128)(2,1)S(1)}, u32[]{:S(2)}, u32[]{:S(2)}) collective-permute-start(bf16[1,512,256]{1,2,0:T(8,128)(2,1)S(1)} %broadcast_select_fusion.4), channel_id=1, source_target_pairs={{0,16},{4,20},{8,24},{12,28},{16,0},{20,4},{24,8},{28,12},{1,17},{... | collective-permute-start | bytes 786440 | tf_op jit(solution)/shard_map/ppermute | solution.py:12
  38.8 7.8 %collective-permute-start.5 = (bf16[1,512,256]{1,2,0:T(8,128)(2,1)S(1)}, bf16[1,512,256]{1,2,0:T(8,128)(2,1)S(1)}, u32[]{:S(2)}, u32[]{:S(2)}) collective-permute-start(bf16[1,512,256]{1,2,0:T(8,128)(2,1)S(1)} %broadcast_select_fusion.6), channel_id=1, source_target_pairs={{0,8},{4,12},{8,0},{12,4},{16,24},{20,28},{24,16},{28,20},{1,9},{5... | collective-permute-start | bytes 786440 | tf_op jit(solution)/shard_map/ppermute | solution.py:12
  46.6 6.9 %collective-permute-start.6 = (bf16[1,512,256]{1,2,0:T(8,128)(2,1)S(1)}, bf16[1,512,256]{1,2,0:T(8,128)(2,1)S(1)}, u32[]{:S(2)}, u32[]{:S(2)}) collective-permute-start(bf16[1,512,256]{1,2,0:T(8,128)(2,1)S(1)} %broadcast_select_fusion.8), channel_id=1, source_target_pairs={{0,4},{4,0},{8,12},{12,8},{16,20},{20,16},{24,28},{28,24},{1,5},{5... | collective-permute-start | bytes 786440 | tf_op jit(solution)/shard_map/ppermute | solution.py:12
  46.8 10.2 %collective-permute-start = (bf16[512,256]{0,1:T(8,128)(2,1)S(1)}, bf16[512,256]{0,1:T(8,128)(2,1)S(1)}, u32[]{:S(2)}, u32[]{:S(2)}) collective-permute-start(bf16[512,256]{0,1:T(8,128)(2,1)S(1)} %get-tuple-element.117), channel_id=1, source_target_pairs={{0,4},{4,8},{8,12},{12,16},{16,20},{20,24},{24,28},{1,5},{5,9},{9,... | collective-permute-start | bytes 786440 | tf_op jit(solution)/shard_map/ppermute | solution.py:18
  61.9 7.0 %collective-permute-start.8 = (bf16[1,512,256]{1,2,0:T(8,128)(2,1)S(1)}, bf16[1,512,256]{1,2,0:T(8,128)(2,1)S(1)}, u32[]{:S(2)}, u32[]{:S(2)}) collective-permute-start(bf16[1,512,256]{1,2,0:T(8,128)(2,1)S(1)} %get-tuple-element.113), channel_id=1, source_target_pairs={{0,4},{4,0},{8,12},{12,8},{16,20},{20,16},{24,28},{28,24},{1,5},{5... | collective-permute-start | bytes 786440 | tf_op jit(solution)/shard_map/ppermute | solution.py:12
  69.0 8.9 %collective-permute-start.9 = (bf16[1,512,256]{1,2,0:T(8,128)(2,1)S(1)}, bf16[1,512,256]{1,2,0:T(8,128)(2,1)S(1)}, u32[]{:S(2)}, u32[]{:S(2)}) collective-permute-start(bf16[1,512,256]{1,2,0:T(8,128)(2,1)S(1)} %broadcast_select_fusion.9), channel_id=1, source_target_pairs={{0,8},{4,12},{8,0},{12,4},{16,24},{20,28},{24,16},{28,20},{1,9},{5... | collective-permute-start | bytes 786440 | tf_op jit(solution)/shard_map/ppermute | solution.py:12
  77.9 10.1 %collective-permute-start.10 = (bf16[1,512,256]{1,2,0:T(8,128)(2,1)S(1)}, bf16[1,512,256]{1,2,0:T(8,128)(2,1)S(1)}, u32[]{:S(2)}, u32[]{:S(2)}) collective-permute-start(bf16[1,512,256]{1,2,0:T(8,128)(2,1)S(1)} %broadcast_select_fusion.7), channel_id=1, source_target_pairs={{0,16},{4,20},{8,24},{12,28},{16,0},{20,4},{24,8},{28,12},{1,17},{... | collective-permute-start | bytes 786440 | tf_op jit(solution)/shard_map/ppermute | solution.py:12
  88.1 8.7 %collective-permute-start.11 = (bf16[1,512,256]{1,2,0:T(8,128)(2,1)S(1)}, bf16[1,512,256]{1,2,0:T(8,128)(2,1)S(1)}, u32[]{:S(2)}, u32[]{:S(2)}) collective-permute-start(bf16[1,512,256]{1,2,0:T(8,128)(2,1)S(1)} %broadcast_select_fusion.5), channel_id=1, source_target_pairs={{0,4},{4,0},{8,12},{12,8},{16,20},{20,16},{24,28},{28,24},{1,5},{5... | collective-permute-start | bytes 786440 | tf_op jit(solution)/shard_map/ppermute | solution.py:12
  96.8 6.4 %collective-permute-start.12 = (bf16[1,512,256]{1,2,0:T(8,128)(2,1)S(1)}, bf16[1,512,256]{1,2,0:T(8,128)(2,1)S(1)}, u32[]{:S(2)}, u32[]{:S(2)}) collective-permute-start(bf16[1,512,256]{1,2,0:T(8,128)(2,1)S(1)} %broadcast_select_fusion.3), channel_id=1, source_target_pairs={{0,8},{4,12},{8,0},{12,4},{16,24},{20,28},{24,16},{28,20},{1,9},{5... | collective-permute-start | bytes 786440 | tf_op jit(solution)/shard_map/ppermute | solution.py:12
  98.2 8.3 %collective-permute-start.7 = (bf16[512,256]{0,1:T(8,128)(2,1)S(1)}, bf16[512,256]{0,1:T(8,128)(2,1)S(1)}, u32[]{:S(2)}, u32[]{:S(2)}) collective-permute-start(bf16[512,256]{0,1:T(8,128)(2,1)S(1)} %get-tuple-element.114), channel_id=1, source_target_pairs={{4,0},{8,4},{12,8},{16,12},{20,16},{24,20},{28,24},{5,1},{9,5},{13... | collective-permute-start | bytes 786440 | tf_op jit(solution)/shard_map/ppermute | solution.py:18
  103.3 6.4 %collective-permute-start.13 = (bf16[1,512,256]{1,2,0:T(8,128)(2,1)S(1)}, bf16[1,512,256]{1,2,0:T(8,128)(2,1)S(1)}, u32[]{:S(2)}, u32[]{:S(2)}) collective-permute-start(bf16[1,512,256]{1,2,0:T(8,128)(2,1)S(1)} %broadcast_select_fusion.1), channel_id=1, source_target_pairs={{0,4},{4,0},{8,12},{12,8},{16,20},{20,16},{24,28},{28,24},{1,5},{5... | collective-permute-start | bytes 786440 | tf_op jit(solution)/shard_map/ppermute | solution.py:12
where the time goes:
time: 112 us; the launch traced here: 111 us
  waiting for transfers between devices  64.4 us (58%)
  starting transfers between devices  21.1 us (19%)
  local copies, waits for them, and re-layouts  12.3 us (11%)
  matrix products  6.07 us (5%)
  between operations  4.77 us (4%)
  other arithmetic  2.76 us (2%)
    ppermute x12, waiting for transfers between devices, from_partner(): return lax.ppermute(value, axis, pairs)  60.3 us
    ppermute x12, starting transfers between devices, from_partner(): return lax.ppermute(value, axis, pairs)  15.9 us
    ppermute x2, starting transfers between devices, passed_along(): lax.ppermute(value, axis, [(source, source + steps) for source in range(f...  5.16 us
    ppermute x2, waiting for transfers between devices, passed_along(): lax.ppermute(value, axis, [(source, source + steps) for source in range(f...  4.15 us
    gather x6, local copies, waits for them, and re-layouts, sort_sections(): jnp.take(keys_now, jnp.bitwise_xor(element_ids, 1 << bit_number))  3.85 us
    gather x6, local copies, waits for them, and re-layouts, sort_sections(): section_list.append((bit_number, jnp.take(moved_flags, my_places)))  3.64 us
    unnamed x8, local copies, waits for them, and re-layouts  3.58 us
  transfers between devices with their start and end apart: 14, of which 14 were waited for; matrix products, arithmetic and copies ran while one was open for 11% of the time, Pallas kernels for 0%

commit v1 on v0

v1 whole, which is shorter than its diff:
```python
import jax
import jax.numpy as jnp
from jax import lax
from jax.sharding import PartitionSpec as P

BLK = 512


def passed_along(value, axis, steps):
    count = lax.axis_size(axis)
    first, last = (max(0, -steps), min(count, count - steps))
    return lax.ppermute(value, axis, [(source, source + steps) for source in range(first, last)])


def window_block(query_rows, window, grad_rows, has_prev):
    width = query_rows.shape[1]
    span = query_rows.shape[0]
    scale = width ** (-0.5)
    win_keys = window[:, :width]
    win_values = window[:, width:]
    scores = jnp.dot(query_rows, win_keys.T, preferred_element_type=jnp.float32) * scale
    column = jnp.arange(window.shape[0], dtype=jnp.int32)
    allowed = jnp.logical_or(column >= span, has_prev)
    scores = jnp.where(allowed[None, :], scores, -1e30)
    top = jnp.max(scores, axis=1, keepdims=True)
    expon = jnp.exp(scores - top)
    probs = expon / jnp.sum(expon, axis=1, keepdims=True)
    probs_low = probs.astype(jnp.bfloat16)
    attended = jnp.dot(probs_low, win_values, preferred_element_type=jnp.float32).astype(
        jnp.bfloat16
    )
    grad_probs = jnp.dot(grad_rows, win_values.T, preferred_element_type=jnp.float32)
    delta = jnp.sum(probs * grad_probs, axis=1, keepdims=True)
    grad_scores = (probs * (grad_probs - delta) * scale).astype(jnp.bfloat16)
    grad_query = jnp.dot(grad_scores, win_keys, preferred_element_type=jnp.float32).astype(
        jnp.bfloat16
    )
    grad_key = jnp.dot(grad_scores.T, query_rows, preferred_element_type=jnp.float32)
    grad_value = jnp.dot(probs_low.T, grad_rows, preferred_element_type=jnp.float32)
    window_grads = jnp.concatenate([grad_key, grad_value], axis=1).astype(jnp.bfloat16)
    return (attended, grad_query, window_grads)


def routed(blocks, order):
    here, rows, width = blocks.shape
    count = lax.axis_size("seq")
    part = rows // count
    cut = blocks.reshape(here, count, part, width).transpose(1, 0, 2, 3)
    spread = lax.all_to_all(cut, "seq", 0, 0)
    sorted_slices = jnp.take(spread.reshape(count * here, part, width), order, axis=0)
    back = lax.all_to_all(sorted_slices.reshape(count, here, part, width), "seq", 0, 0)
    return back.transpose(1, 0, 2, 3).reshape(here, rows, width)


def body(queries, keys, values, grad_out, block_perm):
    width = queries.shape[1]
    blocks_here = queries.shape[0] // BLK
    seq_index = lax.axis_index("seq")
    query_blocks = queries.reshape(blocks_here, BLK, width)
    grad_blocks = grad_out.reshape(blocks_here, BLK, width)
    pair = jnp.concatenate(
        [keys.reshape(blocks_here, BLK, width), values.reshape(blocks_here, BLK, width)], axis=2
    )
    order = block_perm[0]
    inverse = jnp.argmax(
        order[None, :] == jnp.arange(order.shape[0], dtype=jnp.int32)[:, None], axis=1
    )
    prev_pair = passed_along(pair[blocks_here - 1], "seq", 1)
    far_pair = routed(pair, order)
    previous = jnp.concatenate([prev_pair[None], pair[:-1]], axis=0)
    windows = jnp.concatenate([previous, pair, far_pair], axis=1)
    has_prev = seq_index * blocks_here + jnp.arange(blocks_here, dtype=jnp.int32) > 0

    def one_block(items):
        return window_block(items[0], items[1], items[2], items[3])

    attended, grad_query, window_grads = lax.map(
        one_block, (query_blocks, windows, grad_blocks, has_prev)
    )
    prev_back = passed_along(window_grads[0, :BLK], "seq", -1)
    far_back = routed(window_grads[:, 2 * BLK :], inverse)
    local_part = window_grads[:, BLK : 2 * BLK].astype(jnp.float32)
    prev_moved = jnp.concatenate([window_grads[1:, :BLK], prev_back[None]], axis=0).astype(
        jnp.float32
    )
    far_moved = far_back.astype(jnp.float32)
    total = (
        (local_part + prev_moved + far_moved)
        .astype(jnp.bfloat16)
        .reshape(blocks_here * BLK, 2 * width)
    )
    return (
        attended.reshape(blocks_here * BLK, width),
        grad_query.reshape(blocks_here * BLK, width),
        total[:, :width],
        total[:, width:],
    )


def solution(mesh):
    placed = (
        P("seq", "head"),
        P("seq", "head"),
        P("seq", "head"),
        P("seq", "head"),
        P("head", None),
    )
    return jax.shard_map(
        body,
        mesh=mesh,
        in_specs=placed,
        out_specs=(P("seq", "head"), P("seq", "head"), P("seq", "head"), P("seq", "head")),
        check_vma=False,
    )
```

time: 112 us -> 79 us (0.71)
  waiting for transfers between devices: 64.4 us -> 27.6 us
  other arithmetic: 2.76 us -> 9.27 us
  starting transfers between devices: 21.1 us -> 26.3 us
  local copies, waits for them, and re-layouts: 12.3 us -> 7.22 us
  between operations: 4.77 us -> 0.9 us
    ppermute x12 -> x0, waiting for transfers between devices: 60.3 us -> none  [from_partner(): return lax.ppermute(value, axis, pairs)]
    all_to_all x0 -> x4, starting transfers between devices: none -> 20.9 us  [the longest x2 13.8 us: routed(): spread = lax.all_to_all(cut, 'seq', 0, 0)]
    all_to_all x0 -> x4, waiting for transfers between devices: none -> 18.8 us  [the longest x2 15.4 us: routed(): spread = lax.all_to_all(cut, 'seq', 0, 0)]
    ppermute x12 -> x0, starting transfers between devices: 15.9 us -> none  [from_partner(): return lax.ppermute(value, axis, pairs)]
    gather x12 -> x2, local copies, waits for them, and re-layouts: 7.5 us -> 2.07 us  [routed(): jnp.take(spread.reshape(count * here, part, width), order, axis=0)]
    ppermute x2, waiting for transfers between devices: 4.15 us -> 8.77 us  [passed_along(): lax.ppermute(value, axis, [(source, source + steps) for source in range(f...]
    concatenate x1, other arithmetic: 0.02 us -> 1.8 us  [body(): jnp.concatenate([keys.reshape(blocks_here, BLK, width), values.reshape(bl...]
    reshape x0 -> x2, other arithmetic: none -> 1.58 us  [routed(): sorted_slices.reshape(count, here, part, width)]
  transfers between devices with their start and end apart: 14 -> 6, of which waited for: 14 -> 5; matrix products, arithmetic and copies ran while one was open for 11% -> 10% of each run, Pallas kernels for 0% -> 0%
where the time goes in v1:
time: 79 us; the launch traced here: 78.3 us
  waiting for transfers between devices  27.6 us (35%)
  starting transfers between devices  26.3 us (33%)
  other arithmetic  9.27 us (12%)
  local copies, waits for them, and re-layouts  7.22 us (9%)
  matrix products  7.07 us (9%)
  between operations  0.9 us (1%)
    all_to_all x2, waiting for transfers between devices, routed(): spread = lax.all_to_all(cut, 'seq', 0, 0)  15.4 us
    all_to_all x2, starting transfers between devices, routed(): spread = lax.all_to_all(cut, 'seq', 0, 0)  13.8 us
    ppermute x2, waiting for transfers between devices, passed_along(): lax.ppermute(value, axis, [(source, source + steps) for source in range(f...  8.77 us
    all_to_all x2, starting transfers between devices, routed(): lax.all_to_all(sorted_slices.reshape(count, here, part, width), 'seq', 0, 0)  7.14 us
    ppermute x2, starting transfers between devices, passed_along(): lax.ppermute(value, axis, [(source, source + steps) for source in range(f...  5.35 us
    unnamed x32, local copies, waits for them, and re-layouts  4.16 us
    all_to_all x2, waiting for transfers between devices, routed(): lax.all_to_all(sorted_slices.reshape(count, here, part, width), 'seq', 0, 0)  3.41 us
    dot_general x1, matrix products, window_block(): jnp.dot(probs_low, win_values, preferred_element_type=jnp.float32)  2.49 us
  transfers between devices with their start and end apart: 6, of which 5 were waited for; matrix products, arithmetic and copies ran while one was open for 10% of the time, Pallas kernels for 0%

profile of v1, /device:TPU:0, one launch (start us, length us, event | category | flops | bytes accessed | tf_op | source)
XLA Modules:
  0.0 78.3 jit_solution(13332705726463387502)
XLA Ops:
  0.6 0.0 copy-start
  0.6 0.0 copy-start.10
  0.7 0.0 copy-start.9
  0.7 0.0 copy-start.13
  0.7 0.0 copy-start.12
  0.7 1.8 %pad_maximum_fusion.1 = bf16[8,1,64,256]{3,2,1,0:T(8,128)(2,1)} fusion(bf16[8,1,64,128]{3,2,1,0:T(8,128)(2,1)} %bitcast.62, bf16[8,1,64,128]{3,2,1,0:T(8,128)(2,1)} %bitcast.65), kind=kLoop, calls=%fused_computation.38 | loop fusion | flops 524288 | bytes 524288 | tf_op jit(solution)/shard_map/concatenate | solution.py:61
  2.5 7.3 %all-to-all-start = ((bf16[8,1,64,256]{3,2,1,0:T(8,128)(2,1)}), bf16[8,1,64,256]{3,2,1,0:T(8,128)(2,1)S(1)}, u32[]{:S(2)}, u32[]{:S(2)}) async-start(bf16[8,1,64,256]{3,2,1,0:T(8,128)(2,1)} %pad_maximum_fusion.1), calls=%async_computation | async-start | bytes 524288 | tf_op jit(solution)/shard_map/all_to_all | solution.py:49
  9.8 0.7 compare_select_fusion.1
  10.5 0.7 compare_and_fusion.1
  11.1 7.6 %all-to-all-done = bf16[8,1,64,256]{3,2,1,0:T(8,128)(2,1)S(1)} async-done(((bf16[8,1,64,256]{3,2,1,0:T(8,128)(2,1)}), bf16[8,1,64,256]{3,2,1,0:T(8,128)(2,1)S(1)}, u32[]{:S(2)}, u32[]{:S(2)}) %all-to-all-start) | async-done | bytes 262176 | tf_op jit(solution)/shard_map/all_to_all | solution.py:49
  18.7 0.6 gather_fusion
  19.3 0.8 %select_bitcast_fusion.1 = bf16[8,1,64,256]{3,2,1,0:T(8,128)(2,1)} fusion(bf16[8,64,256]{2,1,0:T(8,128)(2,1)S(1)} %gather_fusion, pred[8]{0:T(512)(128)(4,1)S(1)} %compare_and_fusion.1), kind=kLoop, calls=%fused_computation.40 | loop fusion | flops 131072 | bytes 524296 | tf_op jit(solution)/shard_map/reshape | solution.py:51
  20.1 3.6 %all-to-all-start.1 = ((bf16[8,1,64,256]{3,2,1,0:T(8,128)(2,1)}), bf16[8,1,64,256]{3,2,1,0:T(8,128)(2,1)S(1)}, u32[]{:S(2)}, u32[]{:S(2)}) async-start(bf16[8,1,64,256]{3,2,1,0:T(8,128)(2,1)} %select_bitcast_fusion.1), calls=%async_computation.1 | async-start | bytes 524288 | tf_op jit(solution)/shard_map/all_to_all | solution.py:51
  23.7 1.0 %maximum_bitcast_fusion.1 = bf16[512,256]{1,0:T(8,128)(2,1)S(1)} fusion(bf16[1,512,128]{2,1,0:T(8,128)(2,1)} %bitcast.63, bf16[1,512,128]{2,1,0:T(8,128)(2,1)} %bitcast.66), kind=kLoop, calls=%fused_computation.37 | loop fusion | flops 524288 | bytes 524288 | tf_op jit(solution)/shard_map/squeeze | solution.py:68
  24.7 3.9 %collective-permute-start = (bf16[512,256]{1,0:T(8,128)(2,1)S(1)}, bf16[512,256]{1,0:T(8,128)(2,1)S(1)}, u32[]{:S(2)}, u32[]{:S(2)}) collective-permute-start(bf16[512,256]{1,0:T(8,128)(2,1)S(1)} %maximum_bitcast_fusion.1), channel_id=1, source_target_pairs={{0,4},{4,8},{8,12},{12,16},{16,20},{20,24},{24,28},{1,5},{5,9},{9,... | collective-permute-start | bytes 786440 | tf_op jit(solution)/shard_map/ppermute | solution.py:12
  28.6 0.0 copy-done.13
  28.6 0.6 iota_reduce_fusion
  29.3 0.0 copy-start.14
  29.3 4.8 %collective-permute-done = bf16[512,256]{1,0:T(8,128)(2,1)S(1)} collective-permute-done((bf16[512,256]{1,0:T(8,128)(2,1)S(1)}, bf16[512,256]{1,0:T(8,128)(2,1)S(1)}, u32[]{:S(2)}, u32[]{:S(2)}) %collective-permute-start) | collective-permute-done | bytes 262176 | tf_op jit(solution)/shard_map/ppermute | solution.py:12
  34.1 0.0 all-to-all-done.1
  34.1 0.0 copy-done.10
  34.1 0.0 copy-done.9
  34.1 0.1 maximum_bitcast_fusion
  34.2 0.0 copy-done.12
  34.2 0.0 copy-start.5
  34.2 1.2 %fusion.22 = (f32[512]{0:T(512)S(1)}, f32[1536,512]{1,0:T(8,128)S(1)}) fusion(bf16[512,128]{1,0:T(8,128)(2,1)S(1)} %copy-done.12, bf16[1536,256]{1,0:T(8,128)(2,1)S(1)} %maximum_bitcast_fusion, pred[1536]{0:T(1024)(128)(4,1)S(1)} %fusion.18), kind=kOutput, calls=%fused_computation.52 | convolution fusion | flops 203685376 | bytes 3674112 | tf_op jit(solution)/shard_map/while/body/eval_jaxpr/dot_general | solution.py:21
  35.4 0.5 fusion.4
  35.9 0.0 copy-done.5
  35.9 0.0 copy-done
  35.9 0.7 fusion.1
  36.6 0.7 fusion.7
  37.4 0.0 copy-start.7
  37.4 0.9 %fusion.3 = bf16[512,1536]{0,1:T(8,128)(2,1)S(1)} fusion(f32[512,1536]{0,1:T(8,128)S(1)} %get-tuple-element.54, f32[512]{0:T(512)S(1)} %get-tuple-element.53, f32[512]{0:T(512)S(1)} %fusion.4, f32[1536,512]{1,0:T(8,128)S(1)} %get-tuple-element.52, f32[512]{0:T(512)S(1)} %get-tuple-element.51), kind=kLoop, calls=%fused_computation.10 | loop fusion | flops 4718592 | bytes 7870464 | tf_op jit(solution)/shard_map/while/body/eval_jaxpr/convert_element_type | solution.py:34
  38.2 0.0 copy-start.1
  38.3 1.1 %copy-done.1 = bf16[512,1536]{0,1:T(8,128)(2,1)} copy-done((bf16[512,1536]{0,1:T(8,128)(2,1)}, bf16[512,1536]{0,1:T(8,128)(2,1)S(1)}, u32[]{:S(2)}) %copy-start.1) | copy-done | bytes 1572888
  39.4 0.6 fusion.6
  40.0 0.0 copy-done.7
  40.1 0.0 copy-start.3
  40.1 0.8 copy-done.3
  40.8 0.7 fusion.16
  41.6 0.8 %copy.24 = bf16[1,512,256]{2,1,0:T(8,128)(2,1)} copy(bf16[1,512,256]{1,2,0:T(8,128)(2,1)S(1)} %get-tuple-element.48) | data formatting | bytes 524288 | tf_op jit(solution)/shard_map/slice | solution.py:81
  42.4 6.5 %all-to-all-start.2 = ((bf16[8,1,64,256]{3,2,1,0:T(8,128)(2,1)}), bf16[8,1,64,256]{3,2,1,0:T(8,128)(2,1)S(1)}, u32[]{:S(2)}, u32[]{:S(2)}) async-start(bf16[8,1,64,256]{3,2,1,0:T(8,128)(2,1)} %bitcast.71), calls=%async_computation.2 | async-start | bytes 524288 | tf_op jit(solution)/shard_map/all_to_all | solution.py:49
  48.9 0.0 copy-done.14
  48.9 0.7 compare_and_fusion
  49.6 7.8 %all-to-all-done.2 = bf16[8,1,64,256]{3,2,1,0:T(8,128)(2,1)S(1)} async-done(((bf16[8,1,64,256]{3,2,1,0:T(8,128)(2,1)}), bf16[8,1,64,256]{3,2,1,0:T(8,128)(2,1)S(1)}, u32[]{:S(2)}, u32[]{:S(2)}) %all-to-all-start.2) | async-done | bytes 262176 | tf_op jit(solution)/shard_map/all_to_all | solution.py:49
  57.4 0.0 copy-start.11
  57.4 0.7 copy-done.11
  58.1 1.5 %gather_fusion.1 = bf16[8,64,256]{2,1,0:T(8,128)(2,1)S(1)} fusion(bf16[8,64,256]{2,1,0:T(8,128)(2,1)} %bitcast.69, s32[1024]{0:T(1024)S(1)} %pad_clamp_fusion), kind=kCustom, calls=%fused_computation.1.clone | custom fusion | bytes 524320 | tf_op jit(solution)/shard_map/jit(_take)/gather | solution.py:50
  59.6 0.8 %select_bitcast_fusion = bf16[8,1,64,256]{3,2,1,0:T(8,128)(2,1)} fusion(bf16[8,64,256]{2,1,0:T(8,128)(2,1)S(1)} %gather_fusion.1, pred[8]{0:T(512)(128)(4,1)S(1)} %compare_and_fusion), kind=kLoop, calls=%fused_computation.39 | loop fusion | flops 131072 | bytes 524296 | tf_op jit(solution)/shard_map/reshape | solution.py:51
  60.4 3.6 %all-to-all-start.3 = ((bf16[8,1,64,256]{3,2,1,0:T(8,128)(2,1)}), bf16[8,1,64,256]{3,2,1,0:T(8,128)(2,1)S(1)}, u32[]{:S(2)}, u32[]{:S(2)}) async-start(bf16[8,1,64,256]{3,2,1,0:T(8,128)(2,1)} %select_bitcast_fusion), calls=%async_computation.3 | async-start | bytes 524288 | tf_op jit(solution)/shard_map/all_to_all | solution.py:51
  63.9 0.0 copy-start.6
  64.0 2.5 %convolution_convert_fusion.3 = bf16[512,128]{1,0:T(8,128)(2,1)} fusion(bf16[1536,256]{1,0:T(8,128)(2,1)} %copy-done.5, f32[1536,512]{1,0:T(8,128)S(1)} %get-tuple-element.52, f32[512]{0:T(512)S(1)} %fusion.4, f32[512]{0:T(512)S(1)} %get-tuple-element.51), kind=kOutput, calls=%fused_computation.19 | convolution fusion | flops 203751424 | bytes 3674112 | tf_op jit(solution)/shard_map/while/body/eval_jaxpr/dot_general | solution.py:29
  66.4 1.4 %collective-permute-start.1 = (bf16[512,256]{0,1:T(8,128)(2,1)}, bf16[512,256]{0,1:T(8,128)(2,1)S(1)}, u32[]{:S(2)}, u32[]{:S(2)}) collective-permute-start(bf16[512,256]{0,1:T(8,128)(2,1)} %get-tuple-element.47), channel_id=1, source_target_pairs={{4,0},{8,4},{12,8},{16,12},{20,16},{24,20},{28,24},{5,1},{9,5},{13... | collective-permute-start | bytes 786440 | tf_op jit(solution)/shard_map/ppermute | solution.py:12
  67.9 0.0 copy-done.2
  67.9 0.0 copy-done.6
  67.9 1.3 %convolution_convert_fusion.2 = bf16[512,128]{1,0:T(8,128)(2,1)} fusion(bf16[512,1536]{0,1:T(8,128)(2,1)S(1)} %copy-done.2, bf16[1536,256]{1,0:T(8,128)(2,1)S(1)} %copy-done.6), kind=kOutput, calls=%fused_computation.18 | convolution fusion | flops 201392128 | bytes 2097152 | tf_op jit(solution)/shard_map/while/body/eval_jaxpr/dot_general | solution.py:35
  69.2 3.4 %all-to-all-done.3 = bf16[8,1,64,256]{3,2,1,0:T(8,128)(2,1)S(1)} async-done(((bf16[8,1,64,256]{3,2,1,0:T(8,128)(2,1)}), bf16[8,1,64,256]{3,2,1,0:T(8,128)(2,1)S(1)}, u32[]{:S(2)}, u32[]{:S(2)}) %all-to-all-start.3) | async-done | bytes 262176 | tf_op jit(solution)/shard_map/all_to_all | solution.py:51
  72.6 0.1 copy.28
  72.7 4.0 %collective-permute-done.1 = bf16[512,256]{0,1:T(8,128)(2,1)S(1)} collective-permute-done((bf16[512,256]{0,1:T(8,128)(2,1)}, bf16[512,256]{0,1:T(8,128)(2,1)S(1)}, u32[]{:S(2)}, u32[]{:S(2)}) %collective-permute-start.1) | collective-permute-done | bytes 262176 | tf_op jit(solution)/shard_map/ppermute | solution.py:12
  76.7 0.0 copy-done.4
  76.7 0.0 copy-done.8
  76.7 0.1 fusion.14
  76.8 0.8 copy.29
  77.6 0.8 copy.30
  (8 shorter events, 0.0 us)
Async XLA Ops:
  0.6 35.2 %copy-start = (bf16[512,128]{1,0:T(8,128)(2,1)S(1)}, bf16[512,128]{1,0:T(8,128)(2,1)}, u32[]{:S(2)}) copy-start(bf16[512,128]{1,0:T(8,128)(2,1)} %param.10) | copy-start | bytes 393220
  0.6 33.4 %copy-start.10 = (bf16[512,128]{1,0:T(8,128)(2,1)S(1)}, bf16[512,128]{1,0:T(8,128)(2,1)}, u32[]{:S(2)}) copy-start(bf16[512,128]{1,0:T(8,128)(2,1)} %param.8) | copy-start | bytes 393220
  0.7 33.4 %copy-start.9 = (bf16[512,128]{1,0:T(8,128)(2,1)S(1)}, bf16[512,128]{1,0:T(8,128)(2,1)}, u32[]{:S(2)}) copy-start(bf16[512,128]{1,0:T(8,128)(2,1)} %param.9) | copy-start | bytes 393220
  0.7 28.0 %copy-start.13 = (s32[1,8]{1,0:T(1,128)S(1)}, s32[1,8]{1,0:T(1,128)}, u32[]{:S(2)}) copy-start(s32[1,8]{1,0:T(1,128)} %param.11) | copy-start | bytes 100
  0.7 33.5 %copy-start.12 = (bf16[512,128]{1,0:T(8,128)(2,1)S(1)}, bf16[512,128]{1,0:T(8,128)(2,1)}, u32[]{:S(2)}) copy-start(bf16[512,128]{1,0:T(8,128)(2,1)} %param.7) | copy-start | bytes 393220
  2.5 16.2 %all-to-all-start = ((bf16[8,1,64,256]{3,2,1,0:T(8,128)(2,1)}), bf16[8,1,64,256]{3,2,1,0:T(8,128)(2,1)S(1)}, u32[]{:S(2)}, u32[]{:S(2)}) async-start(bf16[8,1,64,256]{3,2,1,0:T(8,128)(2,1)} %pad_maximum_fusion.1), calls=%async_computation | async-start | bytes 524288 | tf_op jit(solution)/shard_map/all_to_all | solution.py:49
  20.1 14.0 %all-to-all-start.1 = ((bf16[8,1,64,256]{3,2,1,0:T(8,128)(2,1)}), bf16[8,1,64,256]{3,2,1,0:T(8,128)(2,1)S(1)}, u32[]{:S(2)}, u32[]{:S(2)}) async-start(bf16[8,1,64,256]{3,2,1,0:T(8,128)(2,1)} %select_bitcast_fusion.1), calls=%async_computation.1 | async-start | bytes 524288 | tf_op jit(solution)/shard_map/all_to_all | solution.py:51
  24.7 9.4 %collective-permute-start = (bf16[512,256]{1,0:T(8,128)(2,1)S(1)}, bf16[512,256]{1,0:T(8,128)(2,1)S(1)}, u32[]{:S(2)}, u32[]{:S(2)}) collective-permute-start(bf16[512,256]{1,0:T(8,128)(2,1)S(1)} %maximum_bitcast_fusion.1), channel_id=1, source_target_pairs={{0,4},{4,8},{8,12},{12,16},{16,20},{20,24},{24,28},{1,5},{5,9},{9,... | collective-permute-start | bytes 786440 | tf_op jit(solution)/shard_map/ppermute | solution.py:12
  29.3 19.6 %copy-start.14 = (s32[8]{0:T(128)}, s32[8]{0:T(128)S(1)}, u32[]{:S(2)}) copy-start(s32[8]{0:T(128)S(1)} %get-tuple-element.22) | copy-start | bytes 100
  34.2 1.7 %copy-start.5 = (bf16[1536,256]{1,0:T(8,128)(2,1)}, bf16[1536,256]{1,0:T(8,128)(2,1)S(1)}, u32[]{:S(2)}) copy-start(bf16[1536,256]{1,0:T(8,128)(2,1)S(1)} %maximum_bitcast_fusion) | copy-start | bytes 2359300
  37.4 2.7 %copy-start.7 = (bf16[1,1536,128]{1,2,0:T(8,128)(2,1)}, bf16[1,1536,128]{1,2,0:T(8,128)(2,1)S(1)}, u32[]{:S(2)}) copy-start(bf16[1,1536,128]{1,2,0:T(8,128)(2,1)S(1)} %fusion.7) | copy-start | bytes 1179652
  38.2 1.1 %copy-start.1 = (bf16[512,1536]{0,1:T(8,128)(2,1)}, bf16[512,1536]{0,1:T(8,128)(2,1)S(1)}, u32[]{:S(2)}) copy-start(bf16[512,1536]{0,1:T(8,128)(2,1)S(1)} %fusion.3) | copy-start | bytes 4718596
  40.1 0.8 copy-start.3
  42.4 15.0 %all-to-all-start.2 = ((bf16[8,1,64,256]{3,2,1,0:T(8,128)(2,1)}), bf16[8,1,64,256]{3,2,1,0:T(8,128)(2,1)S(1)}, u32[]{:S(2)}, u32[]{:S(2)}) async-start(bf16[8,1,64,256]{3,2,1,0:T(8,128)(2,1)} %bitcast.71), calls=%async_computation.2 | async-start | bytes 524288 | tf_op jit(solution)/shard_map/all_to_all | solution.py:49
  57.4 0.7 copy-start.11
  60.4 12.2 %all-to-all-start.3 = ((bf16[8,1,64,256]{3,2,1,0:T(8,128)(2,1)}), bf16[8,1,64,256]{3,2,1,0:T(8,128)(2,1)S(1)}, u32[]{:S(2)}, u32[]{:S(2)}) async-start(bf16[8,1,64,256]{3,2,1,0:T(8,128)(2,1)} %select_bitcast_fusion), calls=%async_computation.3 | async-start | bytes 524288 | tf_op jit(solution)/shard_map/all_to_all | solution.py:51
  63.9 3.9 %copy-start.2 = (bf16[512,1536]{0,1:T(8,128)(2,1)S(1)}, bf16[512,1536]{0,1:T(8,128)(2,1)}, u32[]{:S(2)}) copy-start(bf16[512,1536]{0,1:T(8,128)(2,1)} %copy-done.1) | copy-start | bytes 4718596
  63.9 3.9 %copy-start.6 = (bf16[1536,256]{1,0:T(8,128)(2,1)S(1)}, bf16[1536,256]{1,0:T(8,128)(2,1)}, u32[]{:S(2)}) copy-start(bf16[1536,256]{1,0:T(8,128)(2,1)} %copy-done.5) | copy-start | bytes 2359300
  66.4 10.2 %copy-start.4 = (bf16[1,1536,128]{1,2,0:T(8,128)(2,1)S(1)}, bf16[1,1536,128]{1,2,0:T(8,128)(2,1)}, u32[]{:S(2)}) copy-start(bf16[1,1536,128]{1,2,0:T(8,128)(2,1)} %copy-done.3) | copy-start | bytes 1179652
  66.4 10.2 %copy-start.8 = (bf16[1,1536,128]{1,2,0:T(8,128)(2,1)S(1)}, bf16[1,1536,128]{1,2,0:T(8,128)(2,1)}, u32[]{:S(2)}) copy-start(bf16[1,1536,128]{1,2,0:T(8,128)(2,1)} %copy-done.7) | copy-start | bytes 1179652
  66.4 10.2 %collective-permute-start.1 = (bf16[512,256]{0,1:T(8,128)(2,1)}, bf16[512,256]{0,1:T(8,128)(2,1)S(1)}, u32[]{:S(2)}, u32[]{:S(2)}) collective-permute-start(bf16[512,256]{0,1:T(8,128)(2,1)} %get-tuple-element.47), channel_id=1, source_target_pairs={{4,0},{8,4},{12,8},{16,12},{20,16},{24,20},{28,24},{5,1},{9,5},{13... | collective-permute-start | bytes 786440 | tf_op jit(solution)/shard_map/ppermute | solution.py:12

commit v2 on v1

v2 whole, which is shorter than its diff:
```python
import jax
import jax.numpy as jnp
from jax import lax
from jax.experimental import pallas as pl
from jax.experimental.pallas import tpu as pltpu
from jax.sharding import PartitionSpec as P


NEVER = -1e30
NOTE_ROWS = 16
FEW = 8


def passed_along(value, axis, steps):
    count = lax.axis_size(axis)
    first, last = (max(0, -steps), min(count, count - steps))
    return lax.ppermute(value, axis, [(source, source + steps) for source in range(first, last)])


def rows_by_rows(left, right):
    return lax.dot_general(
        left, right, (((1,), (1,)), ((), ())), preferred_element_type=jnp.float32
    )


def times(left, right):
    return jnp.dot(left, right, preferred_element_type=jnp.float32)


def chunks(rows, size):
    return [(place, pl.ds(place * size, size)) for place in range(rows // size)]


def pack_lent(key, value, joint, slices):
    width = key.shape[1]
    for side, array in enumerate((key, value)):
        lanes = slice(side * width, (side + 1) * width)
        joint[:, lanes] = array[...]
        slices[:, :, lanes] = array[...].reshape(slices.shape[0], slices.shape[1], width)


def split_asked(place, query, grad, joint, kept, sent):
    _, width = query.shape
    half, part, _ = kept.shape
    joint[:, :width] = query[...]
    joint[:, width:] = grad[...]
    for step in range(half):
        for flip, out in enumerate((kept, sent)):
            target = 2 * step + ((place[0] & 1) ^ flip)
            start = pl.multiple_of(target * part, part)
            out[step, :, :width] = query[pl.ds(start, part), :]
            out[step, :, width:] = grad[pl.ds(start, part), :]


def regroup(place, kept, got, *outs):
    for step, out in enumerate(outs):
        source = (place[0] // 2) ^ step
        out[0] = kept[source]
        out[1] = got[source]


def near_statistics(place, query, grad, key, value, previous, level_out, delta_out):
    rows, width = query.shape
    scale = width ** (-0.5)
    has_prev = place[0] > 0
    for _, cut in chunks(rows, 2 * width):
        scores = rows_by_rows(key[...], query[cut, :]) * scale
        prev_scores = rows_by_rows(previous[:, :width], query[cut, :]) * scale
        prev_scores = jnp.where(has_prev, prev_scores, NEVER)
        top = jnp.maximum(
            jnp.max(scores, axis=0, keepdims=True), jnp.max(prev_scores, axis=0, keepdims=True)
        )
        expon = jnp.exp(scores - top)
        prev_expon = jnp.exp(prev_scores - top)
        grad_probs = rows_by_rows(value[...], grad[cut, :])
        prev_grad_probs = rows_by_rows(previous[:, width:], grad[cut, :])
        mass = jnp.sum(expon + prev_expon, axis=0, keepdims=True)
        mixed = jnp.sum(
            expon * grad_probs + prev_expon * prev_grad_probs, axis=0, keepdims=True
        )
        level_out[:, cut] = top + jnp.log(mass)
        delta_out[:, cut] = mixed / mass


def pick_lent(perm, slices, out):
    for target in range(out.shape[0]):
        out[target] = slices[perm[0, target]]


def noted(lines, note, double):
    note[...] = jnp.zeros(note.shape, note.dtype)
    row = 0
    for source, pieces in ((0, 3), (1, 2)):
        values = lines[source : source + 1, :]
        for _ in range(pieces):
            head = values.astype(jnp.bfloat16).astype(jnp.float32)
            values = values - head
            for line in range(values.shape[1] // double):
                note[row : row + 1, :] = head[:, line * double : (line + 1) * double]
                row += 1
    return note[...].astype(jnp.bfloat16)


def pick_asked(place, perm, lines, *arrays):
    half = len(arrays) - 3
    out, scratch, note = arrays[half:]
    part = scratch.shape[1]
    pieces = noted(lines, note, scratch.shape[2])
    for step in range(half):
        scratch[2 * step] = arrays[step][0]
        scratch[2 * step + 1] = arrays[step][1]
    for block in range(2 * half):
        out[perm[0, block], :part, :] = scratch[place[0] ^ block]
        out[block, part:, :] = pieces


def pick_asked_stacked(perm, lines, slices, out, note):
    count, part, double = slices.shape
    pieces = noted(lines, note, double)
    for block in range(count):
        out[perm[0, block], :part, :] = slices[block]
        out[block, part:, :] = pieces


def fetched(brought, rows):
    count, _, double = brought.shape
    part = rows // count
    width = double // 2
    return (
        brought[:, :part, :width].reshape(rows, width),
        brought[:, :part, width:].reshape(rows, width),
    )


def merged(scores, grad_probs, near_level, near_delta):
    top = jnp.maximum(jnp.max(scores, axis=0, keepdims=True), near_level)
    expon = jnp.exp(scores - top)
    kept = jnp.exp(near_level - top)
    mass = kept + jnp.sum(expon, axis=0, keepdims=True)
    mixed = near_delta * kept + jnp.sum(expon * grad_probs, axis=0, keepdims=True)
    share = 1.0 / mass
    return top, expon, mass, share, mixed * share


def far_statistics(query, grad, brought, near_level, near_delta, lines):
    rows, width = query.shape
    scale = width ** (-0.5)
    far_key, far_value = fetched(brought, rows)
    for _, cut in chunks(rows, 2 * width):
        scores = rows_by_rows(far_key, query[cut, :]) * scale
        grad_probs = rows_by_rows(far_value, grad[cut, :])
        top, _, mass, _, delta = merged(scores, grad_probs, near_level[:, cut], near_delta[:, cut])
        lines[0:1, cut] = top + jnp.log(mass)
        lines[1:2, cut] = delta


def query_side(
    place, query, grad, key, value, previous, brought, lines, attended, grad_query, own_grads
):
    rows, width = query.shape
    scale = width ** (-0.5)
    has_prev = place[0] > 0
    sides = (
        (previous[:, :width], previous[:, width:]),
        (key[...], value[...]),
        fetched(brought, rows),
    )
    turned = [(keys.T, values.T) for keys, values in sides]
    grad_key = 0.0
    grad_value = 0.0
    for _, cut in chunks(rows, 2 * width):
        out_turned = 0.0
        grad_turned = 0.0
        for side, (keys, values) in enumerate(sides):
            scores = rows_by_rows(keys, query[cut, :]) * scale
            if side == 0:
                scores = jnp.where(has_prev, scores, NEVER)
            grad_probs = rows_by_rows(values, grad[cut, :])
            probs = jnp.exp(scores - lines[0:1, cut])
            grad_scores = (probs * (grad_probs - lines[1:2, cut])).astype(jnp.bfloat16)
            probs_low = probs.astype(jnp.bfloat16)
            out_turned += times(turned[side][1], probs_low)
            grad_turned += times(turned[side][0], grad_scores)
            if side == 1:
                grad_key += times(grad_scores, query[cut, :])
                grad_value += times(probs_low, grad[cut, :])
        attended[cut, :] = out_turned.T.astype(attended.dtype)
        grad_query[cut, :] = (grad_turned * scale).T.astype(grad_query.dtype)
    own_grads[:, :width] = grad_key * scale
    own_grads[:, width:] = grad_value


def next_asking(place, perm, key, value, asking, lines, own_grads, sums):
    rows, width = key.shape
    scale = width ** (-0.5)
    allowed = place[0] + 1 < perm.shape[1]
    grad_key = 0.0
    grad_value = 0.0
    for _, cut in chunks(rows, 2 * width):
        scores = rows_by_rows(key[...], asking[cut, :width]) * scale
        scores = jnp.where(allowed, scores, NEVER)
        grad_probs = rows_by_rows(value[...], asking[cut, width:])
        probs = jnp.exp(scores - lines[0:1, cut])
        grad_scores = (probs * (grad_probs - lines[1:2, cut])).astype(jnp.bfloat16)
        grad_key += times(grad_scores, asking[cut, :width])
        grad_value += times(probs.astype(jnp.bfloat16), asking[cut, width:])
    sums[:, :width] = own_grads[:, :width] + grad_key * scale
    sums[:, width:] = own_grads[:, width:] + grad_value


def far_asking(place, perm, key, value, asked, sums, key_out, value_out):
    rows, width = key.shape
    scale = width ** (-0.5)
    count = asked.shape[0]
    asker = jnp.int32(0)
    for block in range(count):
        asker = jnp.where(perm[0, block] == place[0], jnp.int32(block), asker)
    note = asked[asker, rows // count :, :].astype(jnp.float32)
    lines = rows // (2 * width)
    query, grad = fetched(asked, rows)
    grad_key = 0.0
    grad_value = 0.0
    for line, _ in chunks(rows, 2 * width):
        pieces = [note[line + lines * piece][None] for piece in range(5)]
        inside = slice(line * 2 * width, (line + 1) * 2 * width)
        scores = rows_by_rows(key[...], query[inside]) * scale
        grad_probs = rows_by_rows(value[...], grad[inside])
        probs = jnp.exp(scores - (pieces[0] + pieces[1] + pieces[2]))
        grad_scores = (probs * (grad_probs - (pieces[3] + pieces[4]))).astype(jnp.bfloat16)
        grad_key += times(grad_scores, query[inside])
        grad_value += times(probs.astype(jnp.bfloat16), grad[inside])
    key_out[...] = (sums[:, :width] + grad_key * scale).astype(key_out.dtype)
    value_out[...] = (sums[:, width:] + grad_value).astype(value_out.dtype)


VMEM = pl.BlockSpec(memory_space=pltpu.VMEM)
SMEM = pl.BlockSpec(memory_space=pltpu.SMEM)


def on_chip(array):
    return pltpu.with_memory_space_constraint(array, pltpu.VMEM)


def call(kernel, outs, *operands, scalars=0, leaving=(), scratch=(), free=False):
    return pl.pallas_call(
        kernel,
        out_shape=tuple(
            jax.ShapeDtypeStruct(shape, dtype) if place in leaving else pltpu.VMEM(shape, dtype)
            for place, (shape, dtype) in enumerate(outs)
        ),
        in_specs=[SMEM] * scalars + [VMEM] * (len(operands) - scalars),
        out_specs=tuple(VMEM for _ in outs),
        scratch_shapes=scratch,
    )(*operands[:scalars], *(operand if free else on_chip(operand) for operand in operands[scalars:]))


def exchanged(cut):
    return lax.all_to_all(cut, "seq", 0, 0)


def layer(query, key, value, grad, perm):
    rows, width = query.shape
    count = lax.axis_size("seq")
    part = rows // count
    place = lax.axis_index("seq").astype(jnp.int32)
    low = jnp.bfloat16
    place = place.reshape(1)
    row = ((1, rows), jnp.float32)
    double = ((rows, 2 * width), jnp.float32)
    half = ((rows, width), low)
    cut = ((count, part, 2 * width), low)
    lent, packed = call(pack_lent, ((double[0], low), cut), key, value, leaving=(1,), free=True)
    lent_before = passed_along(lent, "seq", 1)
    lent_slices = exchanged(packed)
    if count <= FEW:
        quarter = ((count // 2, part, 2 * width), low)
        asked, kept, sent = call(
            split_asked, ((double[0], low), quarter, quarter), place, query, grad, scalars=1
        )
        got = lax.ppermute(sent, "seq", [(source, source ^ 1) for source in range(count)])
        asked_parts = list(
            call(
                regroup,
                (((2, part, 2 * width), low),) * (count // 2),
                place,
                kept,
                got,
                scalars=1,
            )
        )
        for step in range(1, count // 2):
            asked_parts[step] = lax.ppermute(
                asked_parts[step],
                "seq",
                [(source, source ^ (2 * step)) for source in range(count)],
            )
    else:
        asked = jnp.concatenate([query, grad], axis=1)
        asked_slices = exchanged(asked.reshape(cut[0]))
    asked_after = passed_along(asked, "seq", -1)
    near = call(near_statistics, (row, row), place, query, grad, key, value, lent_before, scalars=1)
    lent_sorted = call(pick_lent, (cut,), perm, lent_slices, scalars=1, leaving=(0,))[0]
    brought = exchanged(lent_sorted)
    lines = call(
        far_statistics, (((2, rows), jnp.float32),), query, grad, brought, *near
    )[0]
    noting = ((count, part + NOTE_ROWS, 2 * width), low)
    note = pltpu.VMEM((NOTE_ROWS, 2 * width), jnp.float32)
    if count <= FEW:
        asked_sorted = call(
            pick_asked,
            (noting,),
            place,
            perm,
            lines,
            *asked_parts,
            scalars=2,
            leaving=(0,),
            scratch=[pltpu.VMEM(*cut), note],
        )[0]
    else:
        asked_sorted = call(
            pick_asked_stacked,
            (noting,),
            perm,
            lines,
            asked_slices,
            scalars=1,
            leaving=(0,),
            scratch=[note],
        )[0]
    far_asked = exchanged(asked_sorted)
    lines_after = passed_along(lines, "seq", -1)
    attended, grad_query, own_grads = call(
        query_side,
        (half, half, double),
        place,
        query,
        grad,
        key,
        value,
        lent_before,
        brought,
        lines,
        scalars=1,
        leaving=(0, 1),
    )
    sums = call(
        next_asking,
        (double,),
        place,
        perm,
        key,
        value,
        asked_after,
        lines_after,
        own_grads,
        scalars=2,
    )[0]
    grad_key, grad_value = call(
        far_asking,
        (half, half),
        place,
        perm,
        key,
        value,
        far_asked,
        sums,
        scalars=2,
        leaving=(0, 1),
    )
    return attended, grad_query, grad_key, grad_value


def solution(mesh):
    placed = (
        P("seq", "head"),
        P("seq", "head"),
        P("seq", "head"),
        P("seq", "head"),
        P("head", None),
    )
    return jax.shard_map(
        layer,
        mesh=mesh,
        in_specs=placed,
        out_specs=(P("seq", "head"), P("seq", "head"), P("seq", "head"), P("seq", "head")),
        check_vma=False,
    )
```

time: 79 us -> 68.5 us (0.87)
  the two profiles are of different devices: /device:TPU:0 before, /device:TPU:12 now
where the time goes in v2:
time: 68.5 us; the launch traced here: 67.9 us
  starting transfers between devices  25.7 us (38%)
  waiting for transfers between devices  15.7 us (23%)
  blocking collectives  13.1 us (19%)
  Pallas kernels  12.7 us (19%)
  between operations  0.75 us (1%)
    all_to_all x1, blocking collectives, exchanged(): return lax.all_to_all(cut, 'seq', 0, 0)  13.1 us
    pallas_call x10, Pallas kernels, call(): pl.pallas_call(kernel, out_shape=tuple((jax.ShapeDtypeStruct(shape, dtype...  12.7 us
    all_to_all x2, starting transfers between devices, exchanged(): return lax.all_to_all(cut, 'seq', 0, 0)  12.3 us
    ppermute x3, starting transfers between devices, passed_along(): lax.ppermute(value, axis, [(source, source + steps) for source in range(f...  9.18 us
    ppermute x1, waiting for transfers between devices, layer(): lax.ppermute(sent, 'seq', [(source, source ^ 1) for source in range(count)])  8.56 us
    ppermute x3, waiting for transfers between devices, passed_along(): lax.ppermute(value, axis, [(source, source + steps) for source in range(f...  4.23 us
    ppermute x3, starting transfers between devices, layer(): lax.ppermute(asked_parts[step], 'seq', [(source, source ^ 2 * step) for s...  3.55 us
    ppermute x3, waiting for transfers between devices, layer(): lax.ppermute(asked_parts[step], 'seq', [(source, source ^ 2 * step) for s...  2.89 us
  transfers between devices with their start and end apart: 9, of which 4 were waited for; matrix products, arithmetic and copies ran while one was open for 0% of the time, Pallas kernels for 9%

profile of v2, /device:TPU:12, one launch (start us, length us, event | category | flops | bytes accessed | tf_op | source)
XLA Modules:
  0.0 67.9 jit_solution(1831125779505378899)
XLA Ops:
  0.6 1.7 %shard_map.84 = (bf16[512,256]{1,0:T(8,128)(2,1)S(1)}, bf16[8,64,256]{2,1,0:T(8,128)(2,1)}) custom-call(bf16[512,128]{1,0:T(8,128)(2,1)} %key.9, bf16[512,128]{1,0:T(8,128)(2,1)} %value.9), custom_call_target="tpu_custom_call" | custom-call | tf_op jit(solution)/shard_map/pallas_call | solution.py:245
  2.4 13.1 %all_to_all.15.slices = bf16[8,64,256]{2,1,0:T(8,128)(2,1)S(1)} all-to-all(bf16[8,64,256]{2,1,0:T(8,128)(2,1)} %get-tuple-element.21), channel_id=1, replica_groups=mesh['seq'=8,'head'=4] {'seq'}, dimensions={0} | all-to-all | bytes 524288 | tf_op jit(solution)/shard_map/all_to_all | solution.py:258
  15.5 1.4 %shard_map.85 = bf16[8,64,256]{2,1,0:T(8,128)(2,1)} custom-call(s32[1,8]{1,0:T(1,128)} %perm.7, bf16[8,64,256]{2,1,0:T(8,128)(2,1)S(1)} %all_to_all.15.slices), custom_call_target="tpu_custom_call" | custom-call | tf_op jit(solution)/shard_map/pallas_call | solution.py:245
  16.9 0.0 copy-start.2
  16.9 0.0 copy-start.3
  16.9 5.7 %all-to-all-start.1 = ((bf16[8,64,256]{2,1,0:T(8,128)(2,1)}), bf16[8,64,256]{2,1,0:T(8,128)(2,1)S(1)}, u32[]{:S(2)}, u32[]{:S(2)}) async-start(bf16[8,64,256]{2,1,0:T(8,128)(2,1)} %shard_map.85), calls=%async_computation.1 | async-start | bytes 524288 | tf_op jit(solution)/shard_map/all_to_all | solution.py:258
  22.6 3.4 %collective-permute-start = (bf16[512,256]{1,0:T(8,128)(2,1)S(1)}, bf16[512,256]{1,0:T(8,128)(2,1)S(1)}, u32[]{:S(2)}, u32[]{:S(2)}) collective-permute-start(bf16[512,256]{1,0:T(8,128)(2,1)S(1)} %get-tuple-element.20), channel_id=1, source_target_pairs={{0,4},{4,8},{8,12},{12,16},{16,20},{20,24},{24,28},{1,5},{5,9},{9,... | collective-permute-start | bytes 786440 | tf_op jit(solution)/shard_map/ppermute | solution.py:17
  26.0 0.0 copy-done.2
  26.0 0.0 copy-done.3
  26.0 0.1 shard_map.89
  26.1 0.6 collective-permute-start.1
  26.7 8.6 %collective-permute-done.1.got = bf16[4,64,256]{2,1,0:T(8,128)(2,1)S(1)} collective-permute-done((bf16[4,64,256]{2,1,0:T(8,128)(2,1)S(1)}, bf16[4,64,256]{2,1,0:T(8,128)(2,1)S(1)}, u32[]{:S(2)}, u32[]{:S(2)}) %collective-permute-start.1) | collective-permute-done | bytes 131104 | tf_op jit(solution)/shard_map/ppermute | solution.py:280
  35.3 0.0 copy-start
  35.3 0.0 copy-start.1
  35.3 1.2 %collective-permute-start.2 = (bf16[2,64,256]{2,1,0:T(8,128)(2,1)S(1)}, bf16[2,64,256]{2,1,0:T(8,128)(2,1)S(1)}, u32[]{:S(2)}, u32[]{:S(2)}) collective-permute-start(bf16[2,64,256]{2,1,0:T(8,128)(2,1)S(1)} %get-tuple-element.29), channel_id=1, source_target_pairs={{0,8},{4,12},{8,0},{12,4},{16,24},{20,28},{24,16},{28,20},{1,9},{5... | collective-permute-start | bytes 196616 | tf_op jit(solution)/shard_map/ppermute | solution.py:292
  36.5 1.7 %collective-permute-start.3 = (bf16[2,64,256]{2,1,0:T(8,128)(2,1)S(1)}, bf16[2,64,256]{2,1,0:T(8,128)(2,1)S(1)}, u32[]{:S(2)}, u32[]{:S(2)}) collective-permute-start(bf16[2,64,256]{2,1,0:T(8,128)(2,1)S(1)} %get-tuple-element.30), channel_id=1, source_target_pairs={{0,16},{4,20},{8,24},{12,28},{16,0},{20,4},{24,8},{28,12},{1,17},{... | collective-permute-start | bytes 196616 | tf_op jit(solution)/shard_map/ppermute | solution.py:292
  38.2 0.6 collective-permute-start.4
  38.9 0.0 collective-permute-done.previous
  38.9 0.0 copy-done
  38.9 0.0 copy-done.1
  38.9 0.9 %shard_map.86 = (f32[1,512]{1,0:T(1,128)S(1)}, f32[1,512]{1,0:T(1,128)S(1)}) custom-call(s32[1]{0:T(128)} %bitcast.place, bf16[512,128]{1,0:T(8,128)(2,1)S(1)} %copy-done.2, bf16[512,128]{1,0:T(8,128)(2,1)S(1)} %copy-done.3, bf16[512,128]{1,0:T(8,128)(2,1)S(1)} %copy-done, bf16[512,128]{1,0:T(8,128)(2,1)S(1)} %copy-done.1, ...), custom_call_target="tpu_custom_call" | custom-call | tf_op jit(solution)/shard_map/pallas_call | solution.py:245
  39.8 0.0 all-to-all-done.1.brought
  39.8 0.6 shard_map.87.lines
  40.5 0.0 collective-permute-done.2.arrays_1_
  40.5 1.7 %collective-permute-done.3.arrays_2_ = bf16[2,64,256]{2,1,0:T(8,128)(2,1)S(1)} collective-permute-done((bf16[2,64,256]{2,1,0:T(8,128)(2,1)S(1)}, bf16[2,64,256]{2,1,0:T(8,128)(2,1)S(1)}, u32[]{:S(2)}, u32[]{:S(2)}) %collective-permute-start.3) | collective-permute-done | bytes 65568 | tf_op jit(solution)/shard_map/ppermute | solution.py:292
  42.2 1.2 %collective-permute-done.4.arrays_3_ = bf16[2,64,256]{2,1,0:T(8,128)(2,1)S(1)} collective-permute-done((bf16[2,64,256]{2,1,0:T(8,128)(2,1)S(1)}, bf16[2,64,256]{2,1,0:T(8,128)(2,1)S(1)}, u32[]{:S(2)}, u32[]{:S(2)}) %collective-permute-start.4) | collective-permute-done | bytes 65568 | tf_op jit(solution)/shard_map/ppermute | solution.py:292
  43.4 1.5 %shard_map.91 = bf16[8,80,256]{2,1,0:T(8,128)(2,1)} custom-call(s32[1]{0:T(128)} %bitcast.place, s32[1,8]{1,0:T(1,128)} %perm.7, f32[2,512]{1,0:T(2,128)S(1)} %shard_map.87.lines, bf16[2,64,256]{2,1,0:T(8,128)(2,1)S(1)} %get-tuple-element.28.arrays_0_, bf16[2,64,256]{2,1,0:T(8,128)(2,1)S(1)} %collective-permute-done.2.arrays_1_, ...), custom_call_target="tpu_custom_call" | custom-call | tf_op jit(solution)/shard_map/pallas_call | solution.py:245
  44.8 6.6 %all-to-all-start.2 = ((bf16[8,80,256]{2,1,0:T(8,128)(2,1)}), bf16[8,80,256]{2,1,0:T(8,128)(2,1)S(1)}, u32[]{:S(2)}, u32[]{:S(2)}) async-start(bf16[8,80,256]{2,1,0:T(8,128)(2,1)} %shard_map.91), calls=%async_computation.2 | async-start | bytes 655360 | tf_op jit(solution)/shard_map/all_to_all | solution.py:258
  51.5 2.5 %collective-permute-start.5 = (bf16[512,256]{1,0:T(8,128)(2,1)S(1)}, bf16[512,256]{1,0:T(8,128)(2,1)S(1)}, u32[]{:S(2)}, u32[]{:S(2)}) collective-permute-start(bf16[512,256]{1,0:T(8,128)(2,1)S(1)} %get-tuple-element.32), channel_id=1, source_target_pairs={{4,0},{8,4},{12,8},{16,12},{20,16},{24,20},{28,24},{5,1},{9,5},{13... | collective-permute-start | bytes 786440 | tf_op jit(solution)/shard_map/ppermute | solution.py:17
  53.9 3.4 %collective-permute-start.6 = (f32[2,512]{1,0:T(2,128)S(1)}, f32[2,512]{1,0:T(2,128)S(1)}, u32[]{:S(2)}, u32[]{:S(2)}) collective-permute-start(f32[2,512]{1,0:T(2,128)S(1)} %shard_map.87.lines), channel_id=1, source_target_pairs={{4,0},{8,4},{12,8},{16,12},{20,16},{24,20},{28,24},{5,1},{9,5},{13... | collective-permute-start | bytes 12296 | tf_op jit(solution)/shard_map/ppermute | solution.py:17
  57.3 3.0 %shard_map.88 = (bf16[512,128]{1,0:T(8,128)(2,1)}, bf16[512,128]{1,0:T(8,128)(2,1)}, f32[512,256]{1,0:T(8,128)S(1)}) custom-call(s32[1]{0:T(128)} %bitcast.place, bf16[512,128]{1,0:T(8,128)(2,1)S(1)} %copy-done.2, bf16[512,128]{1,0:T(8,128)(2,1)S(1)} %copy-done.3, bf16[512,128]{1,0:T(8,128)(2,1)S(1)} %copy-done, bf16[512,128]{1,0:T(8,128)(2,1)S(1)} %copy-done.1, ...), custom_call_target="tpu_custom_call" | custom-call | tf_op jit(solution)/shard_map/pallas_call | solution.py:245
  60.2 4.2 %collective-permute-done.5.asking = bf16[512,256]{1,0:T(8,128)(2,1)S(1)} collective-permute-done((bf16[512,256]{1,0:T(8,128)(2,1)S(1)}, bf16[512,256]{1,0:T(8,128)(2,1)S(1)}, u32[]{:S(2)}, u32[]{:S(2)}) %collective-permute-start.5) | collective-permute-done | bytes 262176 | tf_op jit(solution)/shard_map/ppermute | solution.py:17
  64.4 0.0 collective-permute-done.6.lines
  64.5 1.4 %shard_map.92.sums = f32[512,256]{1,0:T(8,128)S(1)} custom-call(s32[1]{0:T(128)} %bitcast.place, s32[1,8]{1,0:T(1,128)} %perm.7, bf16[512,128]{1,0:T(8,128)(2,1)S(1)} %copy-done, bf16[512,128]{1,0:T(8,128)(2,1)S(1)} %copy-done.1, bf16[512,256]{1,0:T(8,128)(2,1)S(1)} %collective-permute-done.5.asking, f32[2,512]{1,0:T(2,128)S(1)} %collective-permute-done.6.lines, ...), custom_call_target="tpu_custom_call" | custom-call | tf_op jit(solution)/shard_map/pallas_call | solution.py:245
  65.9 0.0 all-to-all-done.2.asked
  65.9 2.1 %shard_map.93 = (bf16[512,128]{1,0:T(8,128)(2,1)}, bf16[512,128]{1,0:T(8,128)(2,1)}) custom-call(s32[1]{0:T(128)} %bitcast.place, s32[1,8]{1,0:T(1,128)} %perm.7, bf16[512,128]{1,0:T(8,128)(2,1)S(1)} %copy-done, bf16[512,128]{1,0:T(8,128)(2,1)S(1)} %copy-done.1, bf16[8,80,256]{2,1,0:T(8,128)(2,1)S(1)} %all-to-all-done.2.asked, f32[512,256]{1,0:T(8,128)S(1)} %shard_map.92.sums), custom_call_target="tpu_custom_call" | custom-call | tf_op jit(solution)/shard_map/pallas_call | solution.py:245
  (1 shorter events, 0.0 us)
Async XLA Ops:
  16.9 9.1 %copy-start.2 = (bf16[512,128]{1,0:T(8,128)(2,1)S(1)}, bf16[512,128]{1,0:T(8,128)(2,1)}, u32[]{:S(2)}) copy-start(bf16[512,128]{1,0:T(8,128)(2,1)} %query.7) | copy-start | bytes 393220
  16.9 9.1 %copy-start.3 = (bf16[512,128]{1,0:T(8,128)(2,1)S(1)}, bf16[512,128]{1,0:T(8,128)(2,1)}, u32[]{:S(2)}) copy-start(bf16[512,128]{1,0:T(8,128)(2,1)} %grad.7) | copy-start | bytes 393220
  16.9 22.9 %all-to-all-start.1 = ((bf16[8,64,256]{2,1,0:T(8,128)(2,1)}), bf16[8,64,256]{2,1,0:T(8,128)(2,1)S(1)}, u32[]{:S(2)}, u32[]{:S(2)}) async-start(bf16[8,64,256]{2,1,0:T(8,128)(2,1)} %shard_map.85), calls=%async_computation.1 | async-start | bytes 524288 | tf_op jit(solution)/shard_map/all_to_all | solution.py:258
  22.6 16.3 %collective-permute-start = (bf16[512,256]{1,0:T(8,128)(2,1)S(1)}, bf16[512,256]{1,0:T(8,128)(2,1)S(1)}, u32[]{:S(2)}, u32[]{:S(2)}) collective-permute-start(bf16[512,256]{1,0:T(8,128)(2,1)S(1)} %get-tuple-element.20), channel_id=1, source_target_pairs={{0,4},{4,8},{8,12},{12,16},{16,20},{20,24},{24,28},{1,5},{5,9},{9,... | collective-permute-start | bytes 786440 | tf_op jit(solution)/shard_map/ppermute | solution.py:17
  26.1 9.2 %collective-permute-start.1 = (bf16[4,64,256]{2,1,0:T(8,128)(2,1)S(1)}, bf16[4,64,256]{2,1,0:T(8,128)(2,1)S(1)}, u32[]{:S(2)}, u32[]{:S(2)}) collective-permute-start(bf16[4,64,256]{2,1,0:T(8,128)(2,1)S(1)} %get-tuple-element.27), channel_id=1, source_target_pairs={{0,4},{4,0},{8,12},{12,8},{16,20},{20,16},{24,28},{28,24},{1,5},{5... | collective-permute-start | bytes 393224 | tf_op jit(solution)/shard_map/ppermute | solution.py:280
  35.3 3.6 %copy-start = (bf16[512,128]{1,0:T(8,128)(2,1)S(1)}, bf16[512,128]{1,0:T(8,128)(2,1)}, u32[]{:S(2)}) copy-start(bf16[512,128]{1,0:T(8,128)(2,1)} %key.9) | copy-start | bytes 393220
  35.3 3.6 %copy-start.1 = (bf16[512,128]{1,0:T(8,128)(2,1)S(1)}, bf16[512,128]{1,0:T(8,128)(2,1)}, u32[]{:S(2)}) copy-start(bf16[512,128]{1,0:T(8,128)(2,1)} %value.9) | copy-start | bytes 393220
  35.3 5.2 %collective-permute-start.2 = (bf16[2,64,256]{2,1,0:T(8,128)(2,1)S(1)}, bf16[2,64,256]{2,1,0:T(8,128)(2,1)S(1)}, u32[]{:S(2)}, u32[]{:S(2)}) collective-permute-start(bf16[2,64,256]{2,1,0:T(8,128)(2,1)S(1)} %get-tuple-element.29), channel_id=1, source_target_pairs={{0,8},{4,12},{8,0},{12,4},{16,24},{20,28},{24,16},{28,20},{1,9},{5... | collective-permute-start | bytes 196616 | tf_op jit(solution)/shard_map/ppermute | solution.py:292
  36.5 5.7 %collective-permute-start.3 = (bf16[2,64,256]{2,1,0:T(8,128)(2,1)S(1)}, bf16[2,64,256]{2,1,0:T(8,128)(2,1)S(1)}, u32[]{:S(2)}, u32[]{:S(2)}) collective-permute-start(bf16[2,64,256]{2,1,0:T(8,128)(2,1)S(1)} %get-tuple-element.30), channel_id=1, source_target_pairs={{0,16},{4,20},{8,24},{12,28},{16,0},{20,4},{24,8},{28,12},{1,17},{... | collective-permute-start | bytes 196616 | tf_op jit(solution)/shard_map/ppermute | solution.py:292
  38.2 5.2 %collective-permute-start.4 = (bf16[2,64,256]{2,1,0:T(8,128)(2,1)S(1)}, bf16[2,64,256]{2,1,0:T(8,128)(2,1)S(1)}, u32[]{:S(2)}, u32[]{:S(2)}) collective-permute-start(bf16[2,64,256]{2,1,0:T(8,128)(2,1)S(1)} %get-tuple-element.31), channel_id=1, source_target_pairs={{0,24},{4,28},{8,16},{12,20},{16,8},{20,12},{24,0},{28,4},{1,25},{... | collective-permute-start | bytes 196616 | tf_op jit(solution)/shard_map/ppermute | solution.py:292
  44.8 21.0 %all-to-all-start.2 = ((bf16[8,80,256]{2,1,0:T(8,128)(2,1)}), bf16[8,80,256]{2,1,0:T(8,128)(2,1)S(1)}, u32[]{:S(2)}, u32[]{:S(2)}) async-start(bf16[8,80,256]{2,1,0:T(8,128)(2,1)} %shard_map.91), calls=%async_computation.2 | async-start | bytes 655360 | tf_op jit(solution)/shard_map/all_to_all | solution.py:258
  51.5 13.0 %collective-permute-start.5 = (bf16[512,256]{1,0:T(8,128)(2,1)S(1)}, bf16[512,256]{1,0:T(8,128)(2,1)S(1)}, u32[]{:S(2)}, u32[]{:S(2)}) collective-permute-start(bf16[512,256]{1,0:T(8,128)(2,1)S(1)} %get-tuple-element.32), channel_id=1, source_target_pairs={{4,0},{8,4},{12,8},{16,12},{20,16},{24,20},{28,24},{5,1},{9,5},{13... | collective-permute-start | bytes 786440 | tf_op jit(solution)/shard_map/ppermute | solution.py:17
  53.9 10.6 %collective-permute-start.6 = (f32[2,512]{1,0:T(2,128)S(1)}, f32[2,512]{1,0:T(2,128)S(1)}, u32[]{:S(2)}, u32[]{:S(2)}) collective-permute-start(f32[2,512]{1,0:T(2,128)S(1)} %shard_map.87.lines), channel_id=1, source_target_pairs={{4,0},{8,4},{12,8},{16,12},{20,16},{24,20},{28,24},{5,1},{9,5},{13... | collective-permute-start | bytes 12296 | tf_op jit(solution)/shard_map/ppermute | solution.py:17

commit v3 on v2

--- a/solution.py
+++ b/solution.py
@@ -7,7 +7,7 @@
 
 
 NEVER = -1e30
-NOTE_ROWS = 16
+NOTE_ROWS = 8
 FEW = 8
 
 
@@ -46,7 +46,7 @@
     joint[:, width:] = grad[...]
     for step in range(half):
         for flip, out in enumerate((kept, sent)):
-            target = 2 * step + ((place[0] & 1) ^ flip)
+            target = step + half * ((place[0] // half) ^ flip)
             start = pl.multiple_of(target * part, part)
             out[step, :, :width] = query[pl.ds(start, part), :]
             out[step, :, width:] = grad[pl.ds(start, part), :]
@@ -54,7 +54,7 @@
 
 def regroup(place, kept, got, *outs):
     for step, out in enumerate(outs):
-        source = (place[0] // 2) ^ step
+        source = (place[0] % len(outs)) ^ step
         out[0] = kept[source]
         out[1] = got[source]
 
@@ -90,7 +90,7 @@
 def noted(lines, note, double):
     note[...] = jnp.zeros(note.shape, note.dtype)
     row = 0
-    for source, pieces in ((0, 3), (1, 2)):
+    for source, pieces in ((0, 2), (1, 2)):
         values = lines[source : source + 1, :]
         for _ in range(pieces):
             head = values.astype(jnp.bfloat16).astype(jnp.float32)
@@ -107,8 +107,8 @@
     part = scratch.shape[1]
     pieces = noted(lines, note, scratch.shape[2])
     for step in range(half):
-        scratch[2 * step] = arrays[step][0]
-        scratch[2 * step + 1] = arrays[step][1]
+        scratch[step] = arrays[step][0]
+        scratch[half + step] = arrays[step][1]
     for block in range(2 * half):
         out[perm[0, block], :part, :] = scratch[place[0] ^ block]
         out[block, part:, :] = pieces
@@ -221,12 +221,12 @@
     grad_key = 0.0
     grad_value = 0.0
     for line, _ in chunks(rows, 2 * width):
-        pieces = [note[line + lines * piece][None] for piece in range(5)]
+        pieces = [note[line + lines * piece][None] for piece in range(4)]
         inside = slice(line * 2 * width, (line + 1) * 2 * width)
         scores = rows_by_rows(key[...], query[inside]) * scale
         grad_probs = rows_by_rows(value[...], grad[inside])
-        probs = jnp.exp(scores - (pieces[0] + pieces[1] + pieces[2]))
-        grad_scores = (probs * (grad_probs - (pieces[3] + pieces[4]))).astype(jnp.bfloat16)
+        probs = jnp.exp(scores - (pieces[0] + pieces[1]))
+        grad_scores = (probs * (grad_probs - (pieces[2] + pieces[3]))).astype(jnp.bfloat16)
         grad_key += times(grad_scores, query[inside])
         grad_value += times(probs.astype(jnp.bfloat16), grad[inside])
     key_out[...] = (sums[:, :width] + grad_key * scale).astype(key_out.dtype)
@@ -275,9 +275,15 @@
     if count <= FEW:
         quarter = ((count // 2, part, 2 * width), low)
         asked, kept, sent = call(
-            split_asked, ((double[0], low), quarter, quarter), place, query, grad, scalars=1
+            split_asked,
+            ((double[0], low), quarter, quarter),
+            place,
+            query,
+            grad,
+            scalars=1,
+            free=True,
         )
-        got = lax.ppermute(sent, "seq", [(source, source ^ 1) for source in range(count)])
+        got = lax.ppermute(sent, "seq", [(source, source ^ (count // 2)) for source in range(count)])
         asked_parts = list(
             call(
                 regroup,
@@ -292,7 +298,7 @@
             asked_parts[step] = lax.ppermute(
                 asked_parts[step],
                 "seq",
-                [(source, source ^ (2 * step)) for source in range(count)],
+                [(source, source ^ step) for source in range(count)],
             )
     else:
         asked = jnp.concatenate([query, grad], axis=1)

time: 68.5 us -> 70 us (1.022)
  the two profiles are of different devices: /device:TPU:12 before, /device:TPU:0 now
where the time goes in v3:
time: 70 us; the launch traced here: 68.7 us
  starting transfers between devices  23.1 us (33%)
  blocking collectives  16.2 us (23%)
  waiting for transfers between devices  15 us (21%)
  Pallas kernels  13.6 us (19%)
  between operations  0.77 us (1%)
    all_to_all x1, blocking collectives, exchanged(): return lax.all_to_all(cut, 'seq', 0, 0)  16.2 us
    pallas_call x10, Pallas kernels, call(): pl.pallas_call(kernel, out_shape=tuple((jax.ShapeDtypeStruct(shape, dtype...  13.6 us
    all_to_all x2, starting transfers between devices, exchanged(): return lax.all_to_all(cut, 'seq', 0, 0)  8.38 us
    ppermute x1, waiting for transfers between devices, layer(): lax.ppermute(sent, 'seq', [(source, source ^ count // 2) for source in ra...  6.65 us
    ppermute x3, starting transfers between devices, passed_along(): lax.ppermute(value, axis, [(source, source + steps) for source in range(f...  6.5 us
    ppermute x3, starting transfers between devices, layer(): lax.ppermute(asked_parts[step], 'seq', [(source, source ^ step) for sourc...  5.78 us
    ppermute x3, waiting for transfers between devices, passed_along(): lax.ppermute(value, axis, [(source, source + steps) for source in range(f...  4.83 us
    ppermute x3, waiting for transfers between devices, layer(): lax.ppermute(asked_parts[step], 'seq', [(source, source ^ step) for sourc...  3.52 us
  transfers between devices with their start and end apart: 9, of which 4 were waited for; matrix products, arithmetic and copies ran while one was open for 0% of the time, Pallas kernels for 10%

profile of v3, /device:TPU:0, one launch (start us, length us, event | category | flops | bytes accessed | tf_op | source)
XLA Modules:
  0.0 68.7 jit_solution(7517204624776107389)
XLA Ops:
  0.6 1.7 %shard_map.84 = (bf16[512,256]{1,0:T(8,128)(2,1)S(1)}, bf16[8,64,256]{2,1,0:T(8,128)(2,1)}) custom-call(bf16[512,128]{1,0:T(8,128)(2,1)} %key.9, bf16[512,128]{1,0:T(8,128)(2,1)} %value.9), custom_call_target="tpu_custom_call" | custom-call | tf_op jit(solution)/shard_map/pallas_call | solution.py:245
  2.4 16.2 %all_to_all.15.slices = bf16[8,64,256]{2,1,0:T(8,128)(2,1)S(1)} all-to-all(bf16[8,64,256]{2,1,0:T(8,128)(2,1)} %get-tuple-element.21), channel_id=1, replica_groups=mesh['seq'=8,'head'=4] {'seq'}, dimensions={0} | all-to-all | bytes 524288 | tf_op jit(solution)/shard_map/all_to_all | solution.py:258
  18.6 1.4 %shard_map.85 = bf16[8,64,256]{2,1,0:T(8,128)(2,1)} custom-call(s32[1,8]{1,0:T(1,128)} %perm.7, bf16[8,64,256]{2,1,0:T(8,128)(2,1)S(1)} %all_to_all.15.slices), custom_call_target="tpu_custom_call" | custom-call | tf_op jit(solution)/shard_map/pallas_call | solution.py:245
  20.0 3.6 %all-to-all-start.1 = ((bf16[8,64,256]{2,1,0:T(8,128)(2,1)}), bf16[8,64,256]{2,1,0:T(8,128)(2,1)S(1)}, u32[]{:S(2)}, u32[]{:S(2)}) async-start(bf16[8,64,256]{2,1,0:T(8,128)(2,1)} %shard_map.85), calls=%async_computation.1 | async-start | bytes 524288 | tf_op jit(solution)/shard_map/all_to_all | solution.py:258
  23.6 3.9 %collective-permute-start = (bf16[512,256]{1,0:T(8,128)(2,1)S(1)}, bf16[512,256]{1,0:T(8,128)(2,1)S(1)}, u32[]{:S(2)}, u32[]{:S(2)}) collective-permute-start(bf16[512,256]{1,0:T(8,128)(2,1)S(1)} %get-tuple-element.20), channel_id=1, source_target_pairs={{0,4},{4,8},{8,12},{12,16},{16,20},{20,24},{24,28},{1,5},{5,9},{9,... | collective-permute-start | bytes 786440 | tf_op jit(solution)/shard_map/ppermute | solution.py:17
  27.5 0.0 copy-start.2
  27.5 0.0 copy-start.3
  27.5 1.1 %shard_map.89 = (bf16[512,256]{1,0:T(8,128)(2,1)S(1)}, bf16[4,64,256]{2,1,0:T(8,128)(2,1)S(1)}, bf16[4,64,256]{2,1,0:T(8,128)(2,1)S(1)}) custom-call(s32[1]{0:T(128)} %bitcast.place, bf16[512,128]{1,0:T(8,128)(2,1)} %query.7, bf16[512,128]{1,0:T(8,128)(2,1)} %grad.7), custom_call_target="tpu_custom_call" | custom-call | tf_op jit(solution)/shard_map/pallas_call | solution.py:245
  28.6 2.4 %collective-permute-start.1 = (bf16[4,64,256]{2,1,0:T(8,128)(2,1)S(1)}, bf16[4,64,256]{2,1,0:T(8,128)(2,1)S(1)}, u32[]{:S(2)}, u32[]{:S(2)}) collective-permute-start(bf16[4,64,256]{2,1,0:T(8,128)(2,1)S(1)} %get-tuple-element.27), channel_id=1, source_target_pairs={{0,16},{4,20},{8,24},{12,28},{16,0},{20,4},{24,8},{28,12},{1,17},{... | collective-permute-start | bytes 393224 | tf_op jit(solution)/shard_map/ppermute | solution.py:286
  31.1 6.6 %collective-permute-done.1.got = bf16[4,64,256]{2,1,0:T(8,128)(2,1)S(1)} collective-permute-done((bf16[4,64,256]{2,1,0:T(8,128)(2,1)S(1)}, bf16[4,64,256]{2,1,0:T(8,128)(2,1)S(1)}, u32[]{:S(2)}, u32[]{:S(2)}) %collective-permute-start.1) | collective-permute-done | bytes 131104 | tf_op jit(solution)/shard_map/ppermute | solution.py:286
  37.7 0.0 copy-start
  37.7 0.0 copy-start.1
  37.7 1.6 %collective-permute-start.2 = (bf16[2,64,256]{2,1,0:T(8,128)(2,1)S(1)}, bf16[2,64,256]{2,1,0:T(8,128)(2,1)S(1)}, u32[]{:S(2)}, u32[]{:S(2)}) collective-permute-start(bf16[2,64,256]{2,1,0:T(8,128)(2,1)S(1)} %get-tuple-element.29), channel_id=1, source_target_pairs={{0,4},{4,0},{8,12},{12,8},{16,20},{20,16},{24,28},{28,24},{1,5},{5... | collective-permute-start | bytes 196616 | tf_op jit(solution)/shard_map/ppermute | solution.py:298
  39.3 4.2 %collective-permute-start.3 = (bf16[2,64,256]{2,1,0:T(8,128)(2,1)S(1)}, bf16[2,64,256]{2,1,0:T(8,128)(2,1)S(1)}, u32[]{:S(2)}, u32[]{:S(2)}) collective-permute-start(bf16[2,64,256]{2,1,0:T(8,128)(2,1)S(1)} %get-tuple-element.30), channel_id=1, source_target_pairs={{0,8},{4,12},{8,0},{12,4},{16,24},{20,28},{24,16},{28,20},{1,9},{5... | collective-permute-start | bytes 196616 | tf_op jit(solution)/shard_map/ppermute | solution.py:298
  43.5 0.0 collective-permute-start.4
  43.5 0.0 collective-permute-done.previous
  43.5 0.0 copy-done.2
  43.5 0.0 copy-done.3
  43.5 0.0 copy-done
  43.5 0.0 copy-done.1
  43.6 0.9 %shard_map.86 = (f32[1,512]{1,0:T(1,128)S(1)}, f32[1,512]{1,0:T(1,128)S(1)}) custom-call(s32[1]{0:T(128)} %bitcast.place, bf16[512,128]{1,0:T(8,128)(2,1)S(1)} %copy-done.2, bf16[512,128]{1,0:T(8,128)(2,1)S(1)} %copy-done.3, bf16[512,128]{1,0:T(8,128)(2,1)S(1)} %copy-done, bf16[512,128]{1,0:T(8,128)(2,1)S(1)} %copy-done.1, ...), custom_call_target="tpu_custom_call" | custom-call | tf_op jit(solution)/shard_map/pallas_call | solution.py:245
  44.5 0.0 all-to-all-done.1.brought
  44.5 0.6 shard_map.87.lines
  45.2 0.0 collective-permute-done.2.arrays_1_
  45.2 1.0 %collective-permute-done.3.arrays_2_ = bf16[2,64,256]{2,1,0:T(8,128)(2,1)S(1)} collective-permute-done((bf16[2,64,256]{2,1,0:T(8,128)(2,1)S(1)}, bf16[2,64,256]{2,1,0:T(8,128)(2,1)S(1)}, u32[]{:S(2)}, u32[]{:S(2)}) %collective-permute-start.3) | collective-permute-done | bytes 65568 | tf_op jit(solution)/shard_map/ppermute | solution.py:298
  46.2 2.5 %collective-permute-done.4.arrays_3_ = bf16[2,64,256]{2,1,0:T(8,128)(2,1)S(1)} collective-permute-done((bf16[2,64,256]{2,1,0:T(8,128)(2,1)S(1)}, bf16[2,64,256]{2,1,0:T(8,128)(2,1)S(1)}, u32[]{:S(2)}, u32[]{:S(2)}) %collective-permute-start.4) | collective-permute-done | bytes 65568 | tf_op jit(solution)/shard_map/ppermute | solution.py:298
  48.7 1.4 %shard_map.91 = bf16[8,72,256]{2,1,0:T(8,128)(2,1)} custom-call(s32[1]{0:T(128)} %bitcast.place, s32[1,8]{1,0:T(1,128)} %perm.7, f32[2,512]{1,0:T(2,128)S(1)} %shard_map.87.lines, bf16[2,64,256]{2,1,0:T(8,128)(2,1)S(1)} %get-tuple-element.28.arrays_0_, bf16[2,64,256]{2,1,0:T(8,128)(2,1)S(1)} %collective-permute-done.2.arrays_1_, ...), custom_call_target="tpu_custom_call" | custom-call | tf_op jit(solution)/shard_map/pallas_call | solution.py:245
  50.1 4.8 %all-to-all-start.2 = ((bf16[8,72,256]{2,1,0:T(8,128)(2,1)}), bf16[8,72,256]{2,1,0:T(8,128)(2,1)S(1)}, u32[]{:S(2)}, u32[]{:S(2)}) async-start(bf16[8,72,256]{2,1,0:T(8,128)(2,1)} %shard_map.91), calls=%async_computation.2 | async-start | bytes 589824 | tf_op jit(solution)/shard_map/all_to_all | solution.py:258
  54.9 1.3 %collective-permute-start.5 = (bf16[512,256]{1,0:T(8,128)(2,1)S(1)}, bf16[512,256]{1,0:T(8,128)(2,1)S(1)}, u32[]{:S(2)}, u32[]{:S(2)}) collective-permute-start(bf16[512,256]{1,0:T(8,128)(2,1)S(1)} %get-tuple-element.32), channel_id=1, source_target_pairs={{4,0},{8,4},{12,8},{16,12},{20,16},{24,20},{28,24},{5,1},{9,5},{13... | collective-permute-start | bytes 786440 | tf_op jit(solution)/shard_map/ppermute | solution.py:17
  56.2 1.3 %collective-permute-start.6 = (f32[2,512]{1,0:T(2,128)S(1)}, f32[2,512]{1,0:T(2,128)S(1)}, u32[]{:S(2)}, u32[]{:S(2)}) collective-permute-start(f32[2,512]{1,0:T(2,128)S(1)} %shard_map.87.lines), channel_id=1, source_target_pairs={{4,0},{8,4},{12,8},{16,12},{20,16},{24,20},{28,24},{5,1},{9,5},{13... | collective-permute-start | bytes 12296 | tf_op jit(solution)/shard_map/ppermute | solution.py:17
  57.5 3.0 %shard_map.88 = (bf16[512,128]{1,0:T(8,128)(2,1)}, bf16[512,128]{1,0:T(8,128)(2,1)}, f32[512,256]{1,0:T(8,128)S(1)}) custom-call(s32[1]{0:T(128)} %bitcast.place, bf16[512,128]{1,0:T(8,128)(2,1)S(1)} %copy-done.2, bf16[512,128]{1,0:T(8,128)(2,1)S(1)} %copy-done.3, bf16[512,128]{1,0:T(8,128)(2,1)S(1)} %copy-done, bf16[512,128]{1,0:T(8,128)(2,1)S(1)} %copy-done.1, ...), custom_call_target="tpu_custom_call" | custom-call | tf_op jit(solution)/shard_map/pallas_call | solution.py:245
  60.4 4.8 %collective-permute-done.5.asking = bf16[512,256]{1,0:T(8,128)(2,1)S(1)} collective-permute-done((bf16[512,256]{1,0:T(8,128)(2,1)S(1)}, bf16[512,256]{1,0:T(8,128)(2,1)S(1)}, u32[]{:S(2)}, u32[]{:S(2)}) %collective-permute-start.5) | collective-permute-done | bytes 262176 | tf_op jit(solution)/shard_map/ppermute | solution.py:17
  65.2 0.0 collective-permute-done.6.lines
  65.3 1.4 %shard_map.92.sums = f32[512,256]{1,0:T(8,128)S(1)} custom-call(s32[1]{0:T(128)} %bitcast.place, s32[1,8]{1,0:T(1,128)} %perm.7, bf16[512,128]{1,0:T(8,128)(2,1)S(1)} %copy-done, bf16[512,128]{1,0:T(8,128)(2,1)S(1)} %copy-done.1, bf16[512,256]{1,0:T(8,128)(2,1)S(1)} %collective-permute-done.5.asking, f32[2,512]{1,0:T(2,128)S(1)} %collective-permute-done.6.lines, ...), custom_call_target="tpu_custom_call" | custom-call | tf_op jit(solution)/shard_map/pallas_call | solution.py:245
  66.6 0.0 all-to-all-done.2.asked
  66.7 2.1 %shard_map.93 = (bf16[512,128]{1,0:T(8,128)(2,1)}, bf16[512,128]{1,0:T(8,128)(2,1)}) custom-call(s32[1]{0:T(128)} %bitcast.place, s32[1,8]{1,0:T(1,128)} %perm.7, bf16[512,128]{1,0:T(8,128)(2,1)S(1)} %copy-done, bf16[512,128]{1,0:T(8,128)(2,1)S(1)} %copy-done.1, bf16[8,72,256]{2,1,0:T(8,128)(2,1)S(1)} %all-to-all-done.2.asked, f32[512,256]{1,0:T(8,128)S(1)} %shard_map.92.sums), custom_call_target="tpu_custom_call" | custom-call | tf_op jit(solution)/shard_map/pallas_call | solution.py:245
  (1 shorter events, 0.0 us)
Async XLA Ops:
  20.0 24.5 %all-to-all-start.1 = ((bf16[8,64,256]{2,1,0:T(8,128)(2,1)}), bf16[8,64,256]{2,1,0:T(8,128)(2,1)S(1)}, u32[]{:S(2)}, u32[]{:S(2)}) async-start(bf16[8,64,256]{2,1,0:T(8,128)(2,1)} %shard_map.85), calls=%async_computation.1 | async-start | bytes 524288 | tf_op jit(solution)/shard_map/all_to_all | solution.py:258
  23.6 20.0 %collective-permute-start = (bf16[512,256]{1,0:T(8,128)(2,1)S(1)}, bf16[512,256]{1,0:T(8,128)(2,1)S(1)}, u32[]{:S(2)}, u32[]{:S(2)}) collective-permute-start(bf16[512,256]{1,0:T(8,128)(2,1)S(1)} %get-tuple-element.20), channel_id=1, source_target_pairs={{0,4},{4,8},{8,12},{12,16},{16,20},{20,24},{24,28},{1,5},{5,9},{9,... | collective-permute-start | bytes 786440 | tf_op jit(solution)/shard_map/ppermute | solution.py:17
  27.5 16.0 %copy-start.2 = (bf16[512,128]{1,0:T(8,128)(2,1)S(1)}, bf16[512,128]{1,0:T(8,128)(2,1)}, u32[]{:S(2)}) copy-start(bf16[512,128]{1,0:T(8,128)(2,1)} %query.7) | copy-start | bytes 393220
  27.5 16.0 %copy-start.3 = (bf16[512,128]{1,0:T(8,128)(2,1)S(1)}, bf16[512,128]{1,0:T(8,128)(2,1)}, u32[]{:S(2)}) copy-start(bf16[512,128]{1,0:T(8,128)(2,1)} %grad.7) | copy-start | bytes 393220
  28.6 9.1 %collective-permute-start.1 = (bf16[4,64,256]{2,1,0:T(8,128)(2,1)S(1)}, bf16[4,64,256]{2,1,0:T(8,128)(2,1)S(1)}, u32[]{:S(2)}, u32[]{:S(2)}) collective-permute-start(bf16[4,64,256]{2,1,0:T(8,128)(2,1)S(1)} %get-tuple-element.27), channel_id=1, source_target_pairs={{0,16},{4,20},{8,24},{12,28},{16,0},{20,4},{24,8},{28,12},{1,17},{... | collective-permute-start | bytes 393224 | tf_op jit(solution)/shard_map/ppermute | solution.py:286
  37.7 5.8 %copy-start = (bf16[512,128]{1,0:T(8,128)(2,1)S(1)}, bf16[512,128]{1,0:T(8,128)(2,1)}, u32[]{:S(2)}) copy-start(bf16[512,128]{1,0:T(8,128)(2,1)} %key.9) | copy-start | bytes 393220
  37.7 5.8 %copy-start.1 = (bf16[512,128]{1,0:T(8,128)(2,1)S(1)}, bf16[512,128]{1,0:T(8,128)(2,1)}, u32[]{:S(2)}) copy-start(bf16[512,128]{1,0:T(8,128)(2,1)} %value.9) | copy-start | bytes 393220
  37.7 7.4 %collective-permute-start.2 = (bf16[2,64,256]{2,1,0:T(8,128)(2,1)S(1)}, bf16[2,64,256]{2,1,0:T(8,128)(2,1)S(1)}, u32[]{:S(2)}, u32[]{:S(2)}) collective-permute-start(bf16[2,64,256]{2,1,0:T(8,128)(2,1)S(1)} %get-tuple-element.29), channel_id=1, source_target_pairs={{0,4},{4,0},{8,12},{12,8},{16,20},{20,16},{24,28},{28,24},{1,5},{5... | collective-permute-start | bytes 196616 | tf_op jit(solution)/shard_map/ppermute | solution.py:298
  39.3 6.9 %collective-permute-start.3 = (bf16[2,64,256]{2,1,0:T(8,128)(2,1)S(1)}, bf16[2,64,256]{2,1,0:T(8,128)(2,1)S(1)}, u32[]{:S(2)}, u32[]{:S(2)}) collective-permute-start(bf16[2,64,256]{2,1,0:T(8,128)(2,1)S(1)} %get-tuple-element.30), channel_id=1, source_target_pairs={{0,8},{4,12},{8,0},{12,4},{16,24},{20,28},{24,16},{28,20},{1,9},{5... | collective-permute-start | bytes 196616 | tf_op jit(solution)/shard_map/ppermute | solution.py:298
  43.5 5.2 %collective-permute-start.4 = (bf16[2,64,256]{2,1,0:T(8,128)(2,1)S(1)}, bf16[2,64,256]{2,1,0:T(8,128)(2,1)S(1)}, u32[]{:S(2)}, u32[]{:S(2)}) collective-permute-start(bf16[2,64,256]{2,1,0:T(8,128)(2,1)S(1)} %get-tuple-element.31), channel_id=1, source_target_pairs={{0,12},{4,8},{8,4},{12,0},{16,28},{20,24},{24,20},{28,16},{1,13},{... | collective-permute-start | bytes 196616 | tf_op jit(solution)/shard_map/ppermute | solution.py:298
  50.1 16.5 %all-to-all-start.2 = ((bf16[8,72,256]{2,1,0:T(8,128)(2,1)}), bf16[8,72,256]{2,1,0:T(8,128)(2,1)S(1)}, u32[]{:S(2)}, u32[]{:S(2)}) async-start(bf16[8,72,256]{2,1,0:T(8,128)(2,1)} %shard_map.91), calls=%async_computation.2 | async-start | bytes 589824 | tf_op jit(solution)/shard_map/all_to_all | solution.py:258
  54.9 10.3 %collective-permute-start.5 = (bf16[512,256]{1,0:T(8,128)(2,1)S(1)}, bf16[512,256]{1,0:T(8,128)(2,1)S(1)}, u32[]{:S(2)}, u32[]{:S(2)}) collective-permute-start(bf16[512,256]{1,0:T(8,128)(2,1)S(1)} %get-tuple-element.32), channel_id=1, source_target_pairs={{4,0},{8,4},{12,8},{16,12},{20,16},{24,20},{28,24},{5,1},{9,5},{13... | collective-permute-start | bytes 786440 | tf_op jit(solution)/shard_map/ppermute | solution.py:17
  56.2 9.1 %collective-permute-start.6 = (f32[2,512]{1,0:T(2,128)S(1)}, f32[2,512]{1,0:T(2,128)S(1)}, u32[]{:S(2)}, u32[]{:S(2)}) collective-permute-start(f32[2,512]{1,0:T(2,128)S(1)} %shard_map.87.lines), channel_id=1, source_target_pairs={{4,0},{8,4},{12,8},{16,12},{20,16},{24,20},{28,24},{5,1},{9,5},{13... | collective-permute-start | bytes 12296 | tf_op jit(solution)/shard_map/ppermute | solution.py:17
